TPU v7x, 32 devices: a whole 2x2x4 slice. The times are simulated.
32 devices in a mesh: dp: 2 (over x), row: 4 (over z), col: 4 (over y, core).
Axes of the slice: x: 2, y: 2, z: 4, core: 2. Of those that a mesh axis runs over, the one named last changes fastest.
Arguments:
- layer_input: bfloat16 [2048, 2048], P(('dp', 'col'), 'row'), may hold values from -6 to 6
- cotangent: bfloat16 [2048, 2048], P(('dp', 'col'), 'row'), may hold values from -6 to 6
- w_query: bfloat16 [2048, 2048], P('row', 'col'), may hold values from -0.125 to 0.125
- key_matrix: bfloat16 [2048, 1024], P('row', 'col'), may hold values from -0.125 to 0.125
- value_matrix: bfloat16 [2048, 1024], P('row', 'col'), may hold values from -0.125 to 0.125
- w_output: bfloat16 [2048, 2048], P('col', 'row'), may hold values from -1 to 1
- w_gate: bfloat16 [2048, 6144], P('row', 'col'), may hold values from -0.125 to 0.125
- w_up: bfloat16 [2048, 6144], P('row', 'col'), may hold values from -0.125 to 0.125
- w_down: bfloat16 [6144, 2048], P('col', 'row'), may hold values from -0.078125 to 0.078125
- attn_gain: float32 [2048], P('row'), may hold values from 0.5 to 1.5
- mlp_gain: float32 [2048], P('row'), may hold values from 0.5 to 1.5
- query_gain: float32 [128], replicated, may hold values from 0.5 to 1.5
- key_gain: float32 [128], replicated, may hold values from 0.5 to 1.5
- segment_ids: int32 [8, 256], P(('dp', 'row')), may hold values from 0 to 3, never falling along the last dimension, each value on 1 to 128 neighbouring positions
Outputs:
- block_out: bfloat16 [2048, 2048], P(('dp', 'col'), 'row')
- input_grad: float32 [2048, 2048], P(('dp', 'col'), 'row')
- grad_query: float32 [2048, 2048], P('row', 'col')
- grad_key: float32 [2048, 1024], P('row', 'col')
- grad_value: float32 [2048, 1024], P('row', 'col')
- grad_output: float32 [2048, 2048], P('col', 'row')
- grad_gate: float32 [2048, 6144], P('row', 'col')
- grad_up: float32 [2048, 6144], P('row', 'col')
- grad_down: float32 [6144, 2048], P('col', 'row')
- gain_attn: float32 [2048], replicated
- gain_mlp: float32 [2048], replicated
- gain_query: float32 [128], replicated
- gain_key: float32 [128], replicated
All inputs are finite; a program needn't handle non-finite values.
Results may differ from a plain program's by a relative error of at most 0.015.
Values may be sent and summed in bfloat16 or wider, within the bound.
A program may use at most 128 MiB of HBM per device.

v0:
```python
import jax
import jax.numpy as jnp
from jax import lax
from jax.sharding import PartitionSpec as P

MODEL_WIDTH = 2048
HEAD_SIZE = 128


EPSILON = 1e-06
THETA = 1000000.0


def positions_of(segment):
    length = segment.shape[0]
    index = jnp.arange(length, dtype=jnp.int32)
    change = jnp.concatenate(
        [jnp.ones((1,), jnp.int32), (segment[1:] != segment[:-1]).astype(jnp.int32)]
    )
    starts = lax.cummax(jnp.where(change > 0, index, jnp.zeros_like(index)), axis=0)
    return index - starts


def rope_tables(segment, width):
    half = width // 2
    inverse = jnp.power(THETA, -(jnp.arange(half, dtype=jnp.float32) * (2.0 / width)))
    angle = positions_of(segment).astype(jnp.float32)[:, None] * inverse[None, :]
    return (jnp.cos(angle), jnp.sin(angle))


def rotate(field, cosine, sine):
    half = field.shape[-1] // 2
    first = field[..., :half]
    second = field[..., half:]
    cos_b = cosine[:, None, :]
    sin_b = sine[:, None, :]
    return jnp.concatenate(
        [first * cos_b - second * sin_b, second * cos_b + first * sin_b], axis=-1
    )


def unrotate(grad, cosine, sine):
    half = grad.shape[-1] // 2
    first = grad[..., :half]
    second = grad[..., half:]
    cos_b = cosine[:, None, :]
    sin_b = sine[:, None, :]
    return jnp.concatenate(
        [first * cos_b + second * sin_b, second * cos_b - first * sin_b], axis=-1
    )


def head_norm(field, gain):
    scale = lax.rsqrt(jnp.mean(field * field, axis=-1, keepdims=True) + EPSILON)
    unit = field * scale
    return (unit * gain, unit, scale)


def head_norm_back(grad, unit, scale, gain):
    inner = grad * gain
    back = scale * (inner - unit * jnp.mean(inner * unit, axis=-1, keepdims=True))
    return (back, jnp.sum(grad * unit, axis=(0, 1)))


def mix(form, left, right):
    return jnp.einsum(form, left, right, preferred_element_type=jnp.float32)


def score_mask(segment, start, block):
    length = segment.shape[0]
    query_index = start + jnp.arange(block, dtype=jnp.int32)
    key_index = jnp.arange(length, dtype=jnp.int32)
    return (segment[:, None] == segment[None, :]) & (key_index[None, :] <= query_index[:, None])


def attend(query, key_rows, value_rows, segment):
    length, heads, width = query.shape
    groups = key_rows.shape[1]
    group_factor = heads // groups
    block = min(512, length)
    blocks = length // block
    scale = width ** (-0.5)
    grouped = query.reshape(blocks, block, groups, group_factor, width)
    starts = jnp.arange(blocks, dtype=jnp.int32) * block

    def one_block(item):
        query_block, start = item
        scores = mix("qgrd,kgd->grqk", query_block, key_rows) * scale
        allowed = score_mask(segment, start, block)
        scores = jnp.where(allowed[None, None], scores, -1e30)
        top = jnp.max(scores, axis=-1, keepdims=True)
        weights = jnp.exp(scores - top)
        total = jnp.sum(weights, axis=-1, keepdims=True)
        probs = (weights / total).astype(jnp.bfloat16)
        result = mix("grqk,kgd->qgrd", probs, value_rows)
        return (result.astype(jnp.bfloat16), (top + jnp.log(total))[..., 0])

    results, log_total = lax.map(one_block, (grouped, starts))
    return (results.reshape(length, heads * width), log_total)


def attend_back(query, key_rows, value_rows, segment, mixed, grad_mixed, log_total):
    length, heads, width = query.shape
    groups = key_rows.shape[1]
    group_factor = heads // groups
    block = min(512, length)
    blocks = length // block
    scale = width ** (-0.5)
    delta = jnp.sum(
        grad_mixed.astype(jnp.float32).reshape(length, heads, width)
        * mixed.astype(jnp.float32).reshape(length, heads, width),
        axis=-1,
    )
    delta = jnp.transpose(delta.reshape(blocks, block, groups, group_factor), (0, 2, 3, 1))
    grouped = query.reshape(blocks, block, groups, group_factor, width)
    grouped_grad = grad_mixed.reshape(blocks, block, groups, group_factor, width)
    starts = jnp.arange(blocks, dtype=jnp.int32) * block

    def one_block(carry, item):
        grad_keys, value_gradients = carry
        query_block, grad_block, total_block, delta_block, start = item
        scores = mix("qgrd,kgd->grqk", query_block, key_rows) * scale
        allowed = score_mask(segment, start, block)
        scores = jnp.where(allowed[None, None], scores, -1e30)
        probs = jnp.exp(scores - total_block[..., None])
        value_gradients = value_gradients + mix(
            "grqk,qgrd->kgd", probs.astype(jnp.bfloat16), grad_block
        )
        grad_probs = mix("qgrd,kgd->grqk", grad_block, value_rows)
        grad_scores = (probs * (grad_probs - delta_block[..., None])).astype(jnp.bfloat16)
        grad_query = mix("grqk,kgd->qgrd", grad_scores, key_rows) * scale
        grad_keys = grad_keys + mix("grqk,qgrd->kgd", grad_scores, query_block) * scale
        return ((grad_keys, value_gradients), grad_query)

    empty = jnp.zeros((length, groups, width), jnp.float32)
    (grad_keys, value_gradients), grad_query = lax.scan(
        one_block, (empty, empty), (grouped, grouped_grad, log_total, delta, starts)
    )
    return (grad_query.reshape(length, heads, width), grad_keys, value_gradients)


def silu_parts(gate):
    sigma = jax.nn.sigmoid(gate)
    return (gate * sigma, sigma * (1.0 + gate * (1.0 - sigma)))


def matrix_result(left, right, flipped):
    if flipped:
        return lax.dot_general(
            left, right, (((1,), (1,)), ((), ())), preferred_element_type=jnp.float32
        )
    return jnp.dot(left, right, preferred_element_type=jnp.float32)


def weight_term(left, right):
    return lax.dot_general(
        left, right, (((0,), (0,)), ((), ())), preferred_element_type=jnp.float32
    )


def row_stats(partial_value):
    return lax.psum(partial_value, "row")


def gather_cols(piece):
    return lax.all_gather(piece, "col", axis=0, tiled=True)


def gather_rows(piece):
    return lax.all_gather(piece, "row", axis=0, tiled=True)


def row_product(gathered, weight, flipped):
    return lax.psum_scatter(
        matrix_result(gathered, weight, flipped), "row", scatter_dimension=0, tiled=True
    )


def col_sum(gathered, weight, flipped):
    return lax.psum_scatter(
        matrix_result(gathered, weight, flipped), "col", scatter_dimension=0, tiled=True
    )


def per_device(
    layer_input,
    cotangent,
    w_query,
    key_matrix,
    value_matrix,
    w_output,
    w_gate,
    w_up,
    w_down,
    attn_gain,
    mlp_gain,
    query_gain,
    key_gain,
    segment_ids,
):
    segment = segment_ids[0]
    length = segment.shape[0]
    feat_rows = layer_input.shape[1]
    query_width = w_query.shape[1]
    key_width = key_matrix.shape[1]
    ff_local = w_gate.shape[1]
    cosine, sine = rope_tables(segment, HEAD_SIZE)
    w_joint = jnp.concatenate([w_query, key_matrix, value_matrix], axis=1)
    w_pair = jnp.concatenate([w_gate, w_up], axis=1)
    inputs = layer_input.astype(jnp.float32)
    scale_in = lax.rsqrt(row_stats(jnp.sum(inputs * inputs, axis=-1)) / MODEL_WIDTH + EPSILON)[
        :, None
    ]
    unit_in = inputs * scale_in
    normalized_input = (unit_in * attn_gain).astype(jnp.bfloat16)
    gathered_in = gather_cols(normalized_input)
    projected = row_product(gathered_in, w_joint, False)
    query = projected[:, :query_width].reshape(length, query_width // HEAD_SIZE, HEAD_SIZE)
    key_rows = projected[:, query_width : query_width + key_width].reshape(
        length, key_width // HEAD_SIZE, HEAD_SIZE
    )
    value_rows = (
        projected[:, query_width + key_width :]
        .astype(jnp.bfloat16)
        .reshape(length, key_width // HEAD_SIZE, HEAD_SIZE)
    )
    query_norm, query_unit, query_scale = head_norm(query, query_gain)
    key_norm, key_unit, key_scale = head_norm(key_rows, key_gain)
    query_rot = rotate(query_norm, cosine, sine).astype(jnp.bfloat16)
    key_rot = rotate(key_norm, cosine, sine).astype(jnp.bfloat16)
    mixed, log_total = attend(query_rot, key_rot, value_rows, segment)
    gathered_mix = gather_rows(mixed)
    hidden = inputs + col_sum(gathered_mix, w_output, False)
    scale_mid = lax.rsqrt(row_stats(jnp.sum(hidden * hidden, axis=-1)) / MODEL_WIDTH + EPSILON)[
        :, None
    ]
    unit_mid = hidden * scale_mid
    normed_mid = (unit_mid * mlp_gain).astype(jnp.bfloat16)
    gathered_mid = gather_cols(normed_mid)
    joined = row_product(gathered_mid, w_pair, False)
    gate = joined[:, :ff_local]
    upward = joined[:, ff_local:]
    silu, slope = silu_parts(gate)
    active = (silu * upward).astype(jnp.bfloat16)
    gathered_act = gather_rows(active)
    block_out = (hidden + col_sum(gathered_act, w_down, False)).astype(jnp.bfloat16)
    gathered_cot = gather_cols(cotangent)
    grad_active = row_product(gathered_cot, w_down, True)
    grad_down = weight_term(gathered_act, gathered_cot)
    grad_pair_in = jnp.concatenate(
        [
            (grad_active * upward * slope).astype(jnp.bfloat16),
            (grad_active * silu).astype(jnp.bfloat16),
        ],
        axis=1,
    )
    gathered_pair = gather_rows(grad_pair_in)
    grad_mid = col_sum(gathered_pair, w_pair, True)
    grad_pair = weight_term(gathered_mid, gathered_pair)
    inner_mid = grad_mid * mlp_gain
    gain_mid = jnp.sum(grad_mid * unit_mid, axis=0)
    mean_mid = row_stats(jnp.sum(inner_mid * unit_mid, axis=-1))[:, None] / MODEL_WIDTH
    grad_hidden = cotangent.astype(jnp.float32) + scale_mid * (inner_mid - unit_mid * mean_mid)
    grad_attn = grad_hidden.astype(jnp.bfloat16)
    gathered_attn = gather_cols(grad_attn)
    grad_mixed = row_product(gathered_attn, w_output, True).astype(jnp.bfloat16)
    grad_output = weight_term(gathered_mix, gathered_attn)
    grad_query_rot, grad_key_rot, value_gradients = attend_back(
        query_rot, key_rot, value_rows, segment, mixed, grad_mixed, log_total
    )
    grad_query_raw, gain_query = head_norm_back(
        unrotate(grad_query_rot, cosine, sine), query_unit, query_scale, query_gain
    )
    unrotated_key_gradient, gain_key = head_norm_back(
        unrotate(grad_key_rot, cosine, sine), key_unit, key_scale, key_gain
    )
    grad_joint_in = jnp.concatenate(
        [
            grad_query_raw.reshape(length, query_width).astype(jnp.bfloat16),
            unrotated_key_gradient.reshape(length, key_width).astype(jnp.bfloat16),
            value_gradients.reshape(length, key_width).astype(jnp.bfloat16),
        ],
        axis=1,
    )
    gathered_joint = gather_rows(grad_joint_in)
    grad_in_norm = col_sum(gathered_joint, w_joint, True)
    grad_joint = weight_term(gathered_in, gathered_joint)
    grad_joint, grad_output, grad_pair, grad_down = (
        lax.psum(grad_joint.astype(jnp.bfloat16), "dp").astype(jnp.float32),
        lax.psum(grad_output.astype(jnp.bfloat16), "dp").astype(jnp.float32),
        lax.psum(grad_pair.astype(jnp.bfloat16), "dp").astype(jnp.float32),
        lax.psum(grad_down.astype(jnp.bfloat16), "dp").astype(jnp.float32),
    )
    inner_in = grad_in_norm * attn_gain
    gain_in = jnp.sum(grad_in_norm * unit_in, axis=0)
    mean_in = row_stats(jnp.sum(inner_in * unit_in, axis=-1))[:, None] / MODEL_WIDTH
    input_grad = grad_hidden + scale_in * (inner_in - unit_in * mean_in)
    offset = lax.axis_index("row") * feat_rows
    gain_in_full = lax.dynamic_update_slice(
        jnp.zeros((MODEL_WIDTH,), jnp.float32), gain_in, (offset,)
    )
    gain_mid_full = lax.dynamic_update_slice(
        jnp.zeros((MODEL_WIDTH,), jnp.float32), gain_mid, (offset,)
    )
    gain_attn, gain_mlp, gain_q, gain_k = lax.psum(
        (gain_in_full, gain_mid_full, gain_query, gain_key), ("dp", "row", "col")
    )
    return (
        block_out,
        input_grad,
        grad_joint[:, :query_width],
        grad_joint[:, query_width : query_width + key_width],
        grad_joint[:, query_width + key_width :],
        grad_output,
        grad_pair[:, :ff_local],
        grad_pair[:, ff_local:],
        grad_down,
        gain_attn,
        gain_mlp,
        gain_q,
        gain_k,
    )


def solution(mesh):
    return jax.shard_map(
        per_device,
        mesh=mesh,
        in_specs=(
            P(("dp", "col"), "row"),
            P(("dp", "col"), "row"),
            P("row", "col"),
            P("row", "col"),
            P("row", "col"),
            P("col", "row"),
            P("row", "col"),
            P("row", "col"),
            P("col", "row"),
            P("row"),
            P("row"),
            P(),
            P(),
            P(("dp", "row"), None),
        ),
        out_specs=(
            P(("dp", "col"), "row"),
            P(("dp", "col"), "row"),
            P("row", "col"),
            P("row", "col"),
            P("row", "col"),
            P("col", "row"),
            P("row", "col"),
            P("row", "col"),
            P("col", "row"),
            P(),
            P(),
            P(),
            P(),
        ),
        check_vma=False,
    )
```

profile of v0, /device:TPU:0, one launch (start us, length us, event | category | flops | bytes accessed | tf_op | source)
XLA Modules:
  0.0 1177.3 jit_solution(7358234763588839211)
XLA Ops:
  8.5 13.5 %psum.84 = f32[256]{0:T(256)S(1)} all-reduce(f32[256]{0:T(256)S(1)} %fusion.21), channel_id=1, replica_groups=mesh['dp'=2,'row'=4,'col'=4] {'row'}, use_global_device_ids=true, to_apply=%region_1.2 | all-reduce | flops 256 | bytes 2048 | tf_op jit(solution)/shard_map/psum | solution.py:162
  25.0 13.8 %all-gather.9.cloned.1.call-done = bf16[1024,512]{1,0:T(8,128)(2,1)} async-done(((bf16[256,512]{1,0:T(8,128)(2,1)}), bf16[1024,512]{1,0:T(8,128)(2,1)}) %all-gather.9.cloned.1.call-update) | async-done | bytes 1048592 | tf_op jit(solution)/shard_map/all_gather | solution.py:166
  46.0 74.3 %reduce-scatter.9.cloned.1.call-done = f32[256,1024]{1,0:T(8,128)} async-done(((f32[1024,1024]{1,0:T(8,128)}), f32[256,1024]{1,0:T(8,128)}) %reduce-scatter.9.cloned.1.call-update) | async-done | bytes 1048592 | tf_op jit(solution)/shard_map/reduce_scatter | solution.py:174
  130.9 30.6 %all-gather.11.cloned.1.call-done = bf16[1024,512]{0,1:T(8,128)(2,1)} async-done(((bf16[256,512]{0,1:T(8,128)(2,1)}), bf16[1024,512]{0,1:T(8,128)(2,1)}) %all-gather.11.cloned.1.call-update) | async-done | bytes 1048592 | tf_op jit(solution)/shard_map/all_gather | solution.py:170
  165.4 29.0 %reduce-scatter.11.cloned.1.call-done = f32[256,512]{1,0:T(8,128)} async-done(((f32[1024,512]{1,0:T(8,128)}), f32[256,512]{1,0:T(8,128)}) %reduce-scatter.11.cloned.1.call-update) | async-done | bytes 524304 | tf_op jit(solution)/shard_map/reduce_scatter | solution.py:180
  195.6 12.2 %psum.85 = f32[256]{0:T(256)} all-reduce(f32[256]{0:T(256)S(1)} %get-tuple-element.81), channel_id=1, replica_groups=mesh['dp'=2,'row'=4,'col'=4] {'row'}, use_global_device_ids=true, to_apply=%region_11.12 | all-reduce | flops 256 | bytes 2048 | tf_op jit(solution)/shard_map/psum | solution.py:162
  212.5 5.6 fusion.52
  222.3 9.0 all-gather.13.cloned.1.call-done
  231.3 11.0 fusion.50
  242.5 101.9 %reduce-scatter.17.cloned.1.call-done = f32[256,1536]{1,0:T(8,128)} async-done(((f32[1024,1536]{1,0:T(8,128)}), f32[256,1536]{1,0:T(8,128)}) %reduce-scatter.17.cloned.1.call-update) | async-done | bytes 1572880 | tf_op jit(solution)/shard_map/reduce_scatter | solution.py:174
  344.4 214.8 %reduce-scatter.13.cloned.1.call-done = f32[256,3072]{1,0:T(8,128)} async-done(((f32[1024,3072]{1,0:T(8,128)}), f32[256,3072]{1,0:T(8,128)}) %reduce-scatter.13.cloned.1.call-update) | async-done | bytes 3145744 | tf_op jit(solution)/shard_map/reduce_scatter | solution.py:174
  564.8 116.5 %all-gather.19.cloned.1.call-done = bf16[1024,3072]{1,0:T(8,128)(2,1)} async-done(((bf16[256,3072]{1,0:T(8,128)(2,1)}), bf16[1024,3072]{1,0:T(8,128)(2,1)}) %all-gather.19.cloned.1.call-update) | async-done | bytes 6291472 | tf_op jit(solution)/shard_map/all_gather | solution.py:170
  681.3 8.5 fusion.53
  689.8 29.5 %reduce-scatter.19.cloned.1.call-done = f32[256,512]{1,0:T(8,128)} async-done(((f32[1024,512]{1,0:T(8,128)}), f32[256,512]{1,0:T(8,128)}) %reduce-scatter.19.cloned.1.call-update) | async-done | bytes 524304 | tf_op jit(solution)/shard_map/reduce_scatter | solution.py:180
  721.2 12.3 %psum.86 = f32[256]{0:T(256)} all-reduce(f32[256]{0:T(256)} %get-tuple-element.57), channel_id=1, replica_groups=mesh['dp'=2,'row'=4,'col'=4] {'row'}, use_global_device_ids=true, to_apply=%region_17.18 | all-reduce | flops 256 | bytes 2048 | tf_op jit(solution)/shard_map/psum | solution.py:162
  736.8 14.0 %all-gather.21.cloned.1.call-done = bf16[1024,512]{1,0:T(8,128)(2,1)} async-done(((bf16[256,512]{1,0:T(8,128)(2,1)}), bf16[1024,512]{1,0:T(8,128)(2,1)}) %all-gather.21.cloned.1.call-update) | async-done | bytes 1048592 | tf_op jit(solution)/shard_map/all_gather | solution.py:166
  757.7 40.4 %reduce-scatter.21.cloned.1.call-done = f32[256,512]{1,0:T(8,128)} async-done(((f32[1024,512]{1,0:T(8,128)}), f32[256,512]{1,0:T(8,128)}) %reduce-scatter.21.cloned.1.call-update) | async-done | bytes 524304 | tf_op jit(solution)/shard_map/reduce_scatter | solution.py:174
  827.4 44.4 %all-gather.23.cloned.1.call-done = bf16[1024,1024]{1,0:T(8,128)(2,1)} async-done(((bf16[256,1024]{1,0:T(8,128)(2,1)}), bf16[1024,1024]{1,0:T(8,128)(2,1)}) %all-gather.23.cloned.1.call-update) | async-done | bytes 2097168 | tf_op jit(solution)/shard_map/all_gather | solution.py:170
  876.5 59.5 %all-gather.15.cloned.1.call-done = bf16[1024,1536]{1,0:T(8,128)(2,1)} async-done(((bf16[256,1536]{1,0:T(8,128)(2,1)}), bf16[1024,1536]{1,0:T(8,128)(2,1)}) %all-gather.15.cloned.1.call-update) | async-done | bytes 3145744 | tf_op jit(solution)/shard_map/all_gather | solution.py:170
  947.5 7.8 convolution_convert_fusion
  960.5 8.4 reduce-scatter.23.cloned.1.call-done
  970.4 11.6 psum.87
  982.1 37.7 %all-reduce = (f32[2048]{0:T(1024)}, f32[2048]{0:T(1024)}, f32[128]{0:T(128)}, f32[128]{0:T(128)}) all-reduce(f32[2048]{0:T(1024)S(1)} %dynamic_update_slice.15, f32[2048]{0:T(1024)S(1)} %dynamic_update_slice.16, f32[128]{0:T(128)S(1)} %bitcast_reduce_fusion, ...), channel_id=1, replica_groups=mesh['dp'=2,'row'=4,'col'=4] {'dp','row','col'}, use_global_device_ids=true, to_apply=%region_30.31 | all-reduce | flops 4352 | bytes 34816 | tf_op jit(solution)/shard_map/psum | solution.py:305
  1022.1 138.5 %all-reduce.4.cloned.1.call-done = (bf16[512,1024]{1,0:T(8,128)(2,1)}, bf16[512,512]{1,0:T(8,128)(2,1)}, bf16[512,3072]{1,0:T(8,128)(2,1)}, bf16[1536,512]{1,0:T(8,128)(2,1)}) async-done(((bf16[512,1024]{1,0:T(8,128)(2,1)}, bf16[512,512]{1,0:T(8,128)(2,1)}, bf16[512,3072]{1,0:T(8,128)(2,1)}, bf16[1536,512]{1,0:T(8,128)(2,1)}), (bf16[512,1024]{1,0:T(8,128)(2,1)}, bf16[512,512]{1,0:T(8,128)(2,1)}, ...) | async-done | bytes 6291472 | tf_op jit(solution)/shard_map/psum | solution.py:289
  (247 shorter events, 118.0 us)
Async XLA Ops:
  7.2 205.4 %copy-start = (bf16[1536,512]{1,0:T(8,128)(2,1)S(1)}, bf16[1536,512]{1,0:T(8,128)(2,1)}, u32[]{:S(2)}) copy-start(bf16[1536,512]{1,0:T(8,128)(2,1)} %param.22) | copy-start | bytes 4718596
  7.2 31.6 %all-gather.9.cloned.1.call-start = ((), (), s32[]{:S(2)}) async-start(), calls=%async_computation.8 | async-start | bytes 1310720 | tf_op jit(solution)/shard_map/all_gather | solution.py:166
  23.8 96.5 %reduce-scatter.9.cloned.1.call-start = ((), (), s32[]{:S(2)}) async-start(), calls=%async_computation.9 | async-start | bytes 5242880 | tf_op jit(solution)/shard_map/reduce_scatter | solution.py:174
  43.3 78.7 %copy-start.48 = (f32[128]{0:T(128)S(1)}, f32[128]{0:T(128)}, u32[]{:S(2)}) copy-start(f32[128]{0:T(128)} %param.25) | copy-start | bytes 1540
  43.3 118.1 %all-gather.11.cloned.1.call-start = ((), (), s32[]{:S(2)}) async-start(), calls=%async_computation.10 | async-start | bytes 1310720 | tf_op jit(solution)/shard_map/all_gather | solution.py:170
  46.0 80.1 %copy-start.7 = (f32[256,64]{1,0:T(8,128)}, f32[256,64]{1,0:T(8,128)S(1)}, u32[]{:S(2)}) copy-start(f32[256,64]{1,0:T(8,128)S(1)} %get-tuple-element.111) | copy-start | bytes 196612
  130.8 63.6 %reduce-scatter.11.cloned.1.call-start = ((), (), s32[]{:S(2)}) async-start(), calls=%async_computation.11 | async-start | bytes 2621440 | tf_op jit(solution)/shard_map/reduce_scatter | solution.py:180
  164.8 47.8 %all-gather.17.cloned.1.call-start = ((), (), s32[]{:S(2)}) async-start(), calls=%async_computation.16 | async-start | bytes 1310720 | tf_op jit(solution)/shard_map/all_gather | solution.py:166
  165.3 65.9 %all-gather.13.cloned.1.call-start = ((), (), s32[]{:S(2)}) async-start(), calls=%async_computation.12 | async-start | bytes 1310720 | tf_op jit(solution)/shard_map/all_gather | solution.py:166
  208.5 525.7 %copy-start.37 = (f32[256]{0:T(256)}, f32[256]{0:T(256)S(1)}, u32[]{:S(2)}) copy-start(f32[256]{0:T(256)S(1)} %add_rsqrt_fusion.2) | copy-start | bytes 3076
  209.4 135.0 %reduce-scatter.17.cloned.1.call-start = ((), (), s32[]{:S(2)}) async-start(), calls=%async_computation.17 | async-start | bytes 7864320 | tf_op jit(solution)/shard_map/reduce_scatter | solution.py:174
  218.2 341.0 %reduce-scatter.13.cloned.1.call-start = ((), (), s32[]{:S(2)}) async-start(), calls=%async_computation.13 | async-start | bytes 15728640 | tf_op jit(solution)/shard_map/reduce_scatter | solution.py:174
  242.3 439.0 %all-gather.19.cloned.1.call-start = ((), (), s32[]{:S(2)}) async-start(), calls=%async_computation.18 | async-start | bytes 7864320 | tf_op jit(solution)/shard_map/all_gather | solution.py:170
  564.8 154.5 %reduce-scatter.19.cloned.1.call-start = ((), (), s32[]{:S(2)}) async-start(), calls=%async_computation.19 | async-start | bytes 2621440 | tf_op jit(solution)/shard_map/reduce_scatter | solution.py:180
  689.8 61.1 %all-gather.21.cloned.1.call-start = ((), (), s32[]{:S(2)}) async-start(), calls=%async_computation.20 | async-start | bytes 1310720 | tf_op jit(solution)/shard_map/all_gather | solution.py:166
  736.8 61.3 %reduce-scatter.21.cloned.1.call-start = ((), (), s32[]{:S(2)}) async-start(), calls=%async_computation.21 | async-start | bytes 2621440 | tf_op jit(solution)/shard_map/reduce_scatter | solution.py:174
  754.3 117.5 %all-gather.23.cloned.1.call-start = ((), (), s32[]{:S(2)}) async-start(), calls=%async_computation.22 | async-start | bytes 2621440 | tf_op jit(solution)/shard_map/all_gather | solution.py:170
  826.7 109.3 %all-gather.15.cloned.1.call-start = ((), (), s32[]{:S(2)}) async-start(), calls=%async_computation.14 | async-start | bytes 3932160 | tf_op jit(solution)/shard_map/all_gather | solution.py:170
  827.3 141.5 %reduce-scatter.23.cloned.1.call-start = ((), (), s32[]{:S(2)}) async-start(), calls=%async_computation.23 | async-start | bytes 2621440 | tf_op jit(solution)/shard_map/reduce_scatter | solution.py:180
  876.2 143.5 %reduce-scatter.15.cloned.1.call-start = ((), (), s32[]{:S(2)}) async-start(), calls=%async_computation.15 | async-start | bytes 2621440 | tf_op jit(solution)/shard_map/reduce_scatter | solution.py:180
  941.1 219.5 %all-reduce.4.cloned.1.call-start = ((), (), s32[]{:S(2)}) async-start(), calls=%async_computation.24 | async-start | bytes 12582912 | tf_op jit(solution)/shard_map/psum | solution.py:289
  959.6 60.2 %copy-start.5 = (f32[256,512]{1,0:T(8,128)S(1)}, f32[256,512]{1,0:T(8,128)}, u32[]{:S(2)}) copy-start(f32[256,512]{1,0:T(8,128)} %reduce-scatter.19.cloned.1.call-done) | copy-start | bytes 1572868
  959.6 60.2 %copy-start.16 = (bf16[256,512]{1,0:T(8,128)(2,1)S(1)}, bf16[256,512]{1,0:T(8,128)(2,1)}, u32[]{:S(2)}) copy-start(bf16[256,512]{1,0:T(8,128)(2,1)} %param.15) | copy-start | bytes 786436
  959.6 60.2 %copy-start.38 = (f32[256]{0:T(256)S(1)}, f32[256]{0:T(256)}, u32[]{:S(2)}) copy-start(f32[256]{0:T(256)} %copy-done.37) | copy-start | bytes 3076
  (49 other events, 407.0 us)
Sparse Core Ops, SparseCore 0:
  23.9 14.8 all-gather.8
  43.4 76.8 reduce-scatter.8
  131.0 30.4 all-gather.10
  164.9 29.4 reduce-scatter.10
  195.8 16.6 all-gather.16
  214.5 16.6 all-gather.12
  233.6 110.7 reduce-scatter.16
  346.7 212.3 reduce-scatter.12
  564.9 116.3 all-gather.18
  689.9 29.3 reduce-scatter.18
  736.9 13.9 all-gather.20
  754.4 43.6 reduce-scatter.20
  826.9 44.8 all-gather.22
  873.8 62.2 all-gather.14
  939.0 29.8 reduce-scatter.22
  971.8 31.3 reduce-scatter.14
  1006.8 153.7 all-reduce.3
where the time goes:
time: 1180 us
  waiting for transfers between devices  929 us (79%)
  blocking collectives  87.3 us (7%)
  matrix products  69.7 us (6%)
  other arithmetic  37.9 us (3%)
  local copies, waits for them, and re-layouts  37.7 us (3%)
  between operations  14.6 us (1%)
    reduce_scatter x4, waiting for transfers between devices, row_product(): lax.psum_scatter(matrix_result(gathered, weight, flipped), 'row', scatter...  431 us
    all_gather x4, waiting for transfers between devices, gather_rows(): return lax.all_gather(piece, 'row', axis=0, tiled=True)  251 us
    psum x1, waiting for transfers between devices, per_device(): lax.psum(grad_joint.astype(jnp.bfloat16), 'dp').astype(jnp.float32)  138 us
    reduce_scatter x4, waiting for transfers between devices, col_sum(): lax.psum_scatter(matrix_result(gathered, weight, flipped), 'col', scatter...  66.9 us
    psum x4, blocking collectives, row_stats(): return lax.psum(partial_value, 'row')  49.7 us
    all_gather x4, waiting for transfers between devices, gather_cols(): return lax.all_gather(piece, 'col', axis=0, tiled=True)  39.9 us
    psum x1, blocking collectives, per_device(): lax.psum((gain_in_full, gain_mid_full, gain_query, gain_key), ('dp', 'row...  37.7 us
    dot_general x4, matrix products, matrix_result(): return jnp.dot(left, right, preferred_element_type=jnp.float32)  23.7 us
  transfers between devices with their start and end apart: 17, of which 16 were waited for; matrix products, arithmetic and copies ran while one was open for 5% of the time, Pallas kernels for 0%

commit v1 on v0

v1 whole, which is shorter than its diff:
```python
import functools
from types import SimpleNamespace

import jax
import jax.numpy as jnp
from jax import lax
from jax.experimental import pallas as pl
from jax.experimental.pallas import tpu as pltpu
from jax.sharding import PartitionSpec as P

MODEL_WIDTH = 2048
HEAD_SIZE = 128
EPSILON = 1e-06
THETA = 1000000.0
ROWS = 4
COLS = 4
STEP = 32
MESH = pl.DeviceIdType.MESH
VMEM = pltpu.VMEM
DMA = pltpu.SemaphoreType.DMA
BF16 = jnp.bfloat16
F32 = jnp.float32


def remote(src, dst, send, recv, device):
    return pltpu.make_async_remote_copy(
        src_ref=src,
        dst_ref=dst,
        send_sem=send,
        recv_sem=recv,
        device_id=device,
        device_id_type=MESH,
    )


class Here:
    def __init__(self, n_dp):
        self.n_dp = n_dp
        self.dp = lax.axis_index("dp")
        self.z = lax.axis_index("row")
        self.c = lax.axis_index("col")
        self.core = self.c % 2
        self.c_core = self.c + 1 - 2 * self.core
        self.c_y = (self.c + 2) % COLS
        self.inner = (self.z % 3 + 2) // 3
        self.up = (self.dp, self.z + 1, self.c)
        self.down = (self.dp, self.z - 1, self.c)
        self.over_y = (self.dp, self.z, self.c_y)
        self.over_core = (self.dp, self.z, self.c_core)
        self.over_dp = (1 - self.dp, self.z, self.c)

    def group(self, d):
        return ((self.dp + d) % self.n_dp, self.z, self.c)

    def peers(self):
        for dz in range(ROWS):
            for dc in range(COLS):
                if dz or dc:
                    yield dz * COLS + dc, (self.z + dz) % ROWS, (self.c + dc) % COLS

    def others(self):
        for d in range(1, ROWS):
            yield d, (self.z + d) % ROWS, (self.z - d + ROWS) % ROWS

    def row(self, z):
        return (self.dp, z, self.c)


def meet(here, kinds):
    barrier = pltpu.get_barrier_semaphore()

    def signal(device):
        pl.semaphore_signal(barrier, inc=1, device_id=device, device_id_type=MESH)

    count = 0
    if "dp" in kinds:
        for d in range(1, here.n_dp):
            signal(here.group(d))
        count += here.n_dp - 1
    if "plane" in kinds:
        for _, z, c in here.peers():
            signal((here.dp, z, c))
        count += ROWS * COLS - 1
    else:
        if "col" in kinds:
            signal(here.over_y)
            signal(here.over_core)
            count += 2
        if "rows" in kinds:
            for _, z, _ in here.others():
                signal(here.row(z))
            count += ROWS - 1
        elif "line" in kinds:
            pl.when(here.z < ROWS - 1)(lambda: signal(here.up))
            pl.when(here.z > 0)(lambda: signal(here.down))
            count = count + 1 + here.inner
    pl.semaphore_wait(barrier, count)


class Part:
    def __init__(self, args, outs, scratch, kinds, steps):
        self.args, self.outs, self.scratch = args, outs, scratch
        self.kinds, self.steps = kinds, steps


def run_parts(n_dp, call, *parts):
    counts = [(len(p.args), len(p.outs), len(p.scratch)) for p in parts]
    n_in, n_out = sum(c[0] for c in counts), sum(c[1] for c in counts)
    kinds = set().union(*[p.kinds for p in parts])

    def kernel(*refs):
        here = Here(n_dp)
        ins, outs, scratch = refs[:n_in], refs[n_in : n_in + n_out], refs[n_in + n_out :]
        meet(here, kinds)
        live = []
        for part, (a, o, s) in zip(parts, counts):
            live.append(part.steps(here, ins[:a], outs[:o], scratch[:s]))
            ins, outs, scratch = ins[a:], outs[o:], scratch[s:]
        while live:
            live = [g for g in live if next(g, "end") != "end"]

    vmem = pl.BlockSpec(memory_space=VMEM)
    results = pl.pallas_call(
        kernel,
        out_shape=[o for p in parts for o in p.outs],
        in_specs=[vmem] * n_in,
        out_specs=[vmem] * n_out,
        scratch_shapes=[s for p in parts for s in p.scratch],
        compiler_params=pltpu.CompilerParams(
            collective_id=call, has_side_effects=True, vmem_limit_bytes=60 << 20
        ),
        name=f"stage_{call}",
    )(*[x for p in parts for x in p.args])
    split = []
    for _, o, _ in counts:
        split.append(results[:o])
        results = results[o:]
    return split


def chunked(n, fn):
    step = min(STEP, n)

    def body(i, _):
        fn(pl.multiple_of(i * step, step), step)
        return 0

    lax.fori_loop(0, n // step, body, 0)


def at(place, r, step):
    rows, cols = place
    return pl.ds(rows.start + r, step), cols


def tokens_by_row(n):
    return lambda zz, cc: (pl.ds(pl.multiple_of(zz * n, n), n), slice(None))


def tokens_by_col(n):
    return lambda zz, cc: (pl.ds(pl.multiple_of(cc * n, n), n), slice(None))


def whole_plane(n, w):
    return lambda zz, cc: (
        pl.ds(pl.multiple_of(cc * n, n), n),
        pl.ds(pl.multiple_of(zz * w, w), w),
    )


def gather(x, use_z, use_c, stat=None):
    n, w = x.shape
    if use_z and use_c:
        place, shape = whole_plane(n, w), (n * COLS, w * ROWS)
    elif use_z:
        place, shape = tokens_by_row(n), (n * ROWS, w)
    else:
        place, shape = tokens_by_col(n), (n * COLS, w)
    with_stat = stat is not None
    args, outs = [x], [jax.ShapeDtypeStruct(shape, x.dtype)]
    scratch = [DMA((ROWS,))] * 5 + [DMA((2 * ROWS,))] * 2
    kinds = ({"line"} if use_z else set()) | ({"col"} if use_c else set())
    if with_stat:
        args.append(stat)
        outs.append(jax.ShapeDtypeStruct((ROWS * COLS,) + stat.shape, stat.dtype))
        scratch += [DMA((ROWS * COLS,))] * 2
        kinds.add("plane")

    def steps(here, ins, outs, sems):
        z, c = here.z, here.c
        x_ref, o_ref = ins[0], outs[0]
        up_send, down_send, z_recv, y_send, y_recv, c_send, c_recv = sems[:7]

        def slot(zz, cc):
            return o_ref.at[place(zz, cc)]

        def to_up(src, zz, d):
            return remote(src, slot(zz, c), up_send.at[d], z_recv.at[zz], here.up)

        def to_down(src, zz, d):
            return remote(src, slot(zz, c), down_send.at[d], z_recv.at[zz], here.down)

        def to_y(src, zz):
            return remote(src, slot(zz, c), y_send.at[zz], y_recv.at[zz], here.over_y)

        def to_core(src, zz, cc, half):
            k = half * ROWS + zz
            return remote(src, slot(zz, cc), c_send.at[k], c_recv.at[k], here.over_core)

        def arrived(zz, cc, sem):
            remote(slot(zz, cc), slot(zz, cc), y_send.at[0], sem, here.over_y).wait_recv()

        top, low = z < ROWS - 1, z > 0
        if use_z:
            pl.when(top)(lambda: to_up(x_ref, z, 0).start())
            pl.when(low)(lambda: to_down(x_ref, z, 0).start())
        if use_c:
            to_y(x_ref, z).start()
            to_core(x_ref, z, c, 0).start()
        if with_stat:
            st_ref, so_ref = ins[1], outs[1]
            s_send, s_recv = sems[7:]
            me = z * COLS + c
            for k, zz, cc in here.peers():
                remote(
                    st_ref, so_ref.at[me], s_send.at[k], s_recv.at[me], (here.dp, zz, cc)
                ).start()
            so_ref[me] = st_ref[...]
        mine = place(z, c)

        def keep(r, step):
            o_ref[at(mine, r, step)] = x_ref[pl.ds(r, step), :]

        chunked(n, keep)
        yield

        def from_y(zz):
            arrived(zz, here.c_y, y_recv.at[zz])
            to_core(slot(zz, here.c_y), zz, here.c_y, 1).start()

        if use_z:
            for d in range(1, ROWS):
                below, above = z - d, z + d

                def step_below(below=below, d=d):
                    arrived(below, c, z_recv.at[below])
                    pl.when(top)(lambda: to_up(slot(below, c), below, d).start())
                    if use_c:
                        to_y(slot(below, c), below).start()
                        to_core(slot(below, c), below, c, 0).start()

                def step_above(above=above, d=d):
                    arrived(above, c, z_recv.at[above])
                    pl.when(low)(lambda: to_down(slot(above, c), above, d).start())
                    if use_c:
                        to_y(slot(above, c), above).start()
                        to_core(slot(above, c), above, c, 0).start()

                pl.when(below >= 0)(step_below)
                pl.when(above < ROWS)(step_above)
                yield
                if use_c:
                    if d == 1:
                        from_y(z)
                    else:
                        pl.when(z - (d - 1) >= 0)(lambda d=d: from_y(z - (d - 1)))
                        pl.when(z + (d - 1) < ROWS)(lambda d=d: from_y(z + (d - 1)))
                    yield
            if use_c:
                pl.when(z - (ROWS - 1) >= 0)(lambda: from_y(z - (ROWS - 1)))
                pl.when(z + (ROWS - 1) < ROWS)(lambda: from_y(z + (ROWS - 1)))
                yield
        else:
            from_y(z)
            yield

        if use_z:
            pl.when(top)(lambda: to_up(x_ref, z, 0).wait_send())
            pl.when(low)(lambda: to_down(x_ref, z, 0).wait_send())
            for d in range(1, ROWS):
                below, above = z - d, z + d
                pl.when((below >= 0) & top)(
                    lambda below=below, d=d: to_up(slot(below, c), below, d).wait_send()
                )
                pl.when((above < ROWS) & low)(
                    lambda above=above, d=d: to_down(slot(above, c), above, d).wait_send()
                )
        if use_c:
            for d in range(ROWS if use_z else 1):
                zz = (z + d) % ROWS
                to_y(slot(zz, c), zz).wait_send()
                to_core(slot(zz, c), zz, c, 0).wait_send()
                to_core(slot(zz, here.c_y), zz, here.c_y, 1).wait_send()
                arrived(zz, here.c_core, c_recv.at[zz])
                arrived(zz, (here.c_core + 2) % COLS, c_recv.at[ROWS + zz])
        if with_stat:
            for k, zz, cc in here.peers():
                source = zz * COLS + cc
                copy = remote(
                    st_ref, so_ref.at[source], s_send.at[k], s_recv.at[source], (here.dp, zz, cc)
                )
                copy.wait_send()
                copy.wait_recv()

    return Part(args, outs, scratch, kinds, steps)


def row_stats(here):
    sends = [(0, here.z, None, here.z, True)]
    sends += [(d, here.z, here.row(zz), zz, None) for d, zz, _ in here.others()]
    return sends, [(zz, None) for _, zz, _ in here.others()]


def plane_stats(here):
    me = here.z * COLS + here.c
    sends = [(0, me, None, here.c, True)]
    sends += [(k, me, (here.dp, zz, cc), cc, None) for k, zz, cc in here.peers()]
    return sends, [(zz * COLS + cc, None) for _, zz, cc in here.peers()]


def owner_stats(here):
    own = here.c == here.z
    sends = [(0, here.c, (here.dp, here.z, here.z), 0, own)]
    sends += [(d, here.c, (here.dp, zz, here.z), 0, None) for d, zz, _ in here.others()]
    receives = [(here.c, own)] + [((here.c + d) % COLS, None) for d in range(1, COLS)]
    return sends, receives


def send_stats(stat, stat_to):
    count = ROWS * COLS if stat_to is plane_stats else ROWS
    outs = [jax.ShapeDtypeStruct((count,) + stat.shape[1:], stat.dtype)]

    def steps(here, ins, outs, sems):
        (st_ref,), (so_ref,), (s_send, s_recv) = ins, outs, sems
        sends, receives = stat_to(here)

        def copy(k, slot, device, block):
            return remote(
                st_ref.at[block], so_ref.at[slot], s_send.at[k], s_recv.at[slot], device
            )

        for k, slot, device, block, own in sends:

            def keep(block=block, slot=slot):
                so_ref[slot] = st_ref[block]

            def go(k=k, slot=slot, device=device, block=block):
                copy(k, slot, device, block).start()

            if own is None:
                go()
            elif own is True:
                keep()
            else:
                pl.when(own)(keep)
                pl.when(jnp.logical_not(own))(go)
        yield
        for k, slot, device, block, own in sends:
            if own is not True:
                done = functools.partial(copy, k, slot, device, block)
                if own is None:
                    done().wait_send()
                else:
                    pl.when(jnp.logical_not(own))(lambda done=done: done().wait_send())
        for slot, own in receives:
            got = functools.partial(copy, 0, slot, here.over_core, 0)
            if own is None:
                got().wait_recv()
            else:
                pl.when(jnp.logical_not(own))(lambda got=got: got().wait_recv())

    kinds = {"rows"} if stat_to is row_stats else {"plane"}
    return Part([stat], outs, [DMA((count,))] * 2, kinds, steps)


def scatter_sum(p, use_z, use_c, dtype=F32):
    rows, cols = p.shape
    if use_z and use_c:
        n, w = rows // COLS, cols // ROWS
        place = whole_plane(n, w)
    elif use_z:
        n, w = rows // ROWS, cols
        place = tokens_by_row(n)
    else:
        n, w = rows // COLS, cols
        place = tokens_by_col(n)
    blocks = ROWS if use_z else 1
    scratch = []
    if use_c:
        scratch += [VMEM((2 * blocks, n, w), BF16), VMEM((blocks, n, w), BF16)]
        scratch += [VMEM((blocks, n, w), BF16)]
        scratch += [DMA((2 * blocks,))] * 2 + [DMA((blocks,))] * 2
    if use_z:
        scratch += [VMEM((ROWS - 1, n, w), BF16)] + [VMEM((ROWS, n, w), BF16)] * 2
        scratch += [DMA((ROWS,))] * 3
    kinds = ({"line"} if use_z else set()) | ({"col"} if use_c else set())

    def steps(here, ins, outs, refs):
        z, c = here.z, here.c
        (p_ref,), (o_ref,) = ins, outs
        if use_c:
            c_buf, t_buf, y_buf, c_send, c_recv, y_send, y_recv, *refs = refs
        if use_z:
            z_out, z_up, z_down, z_send, up_recv, down_recv = refs
        mirrored = z // 2

        def dest(i):
            if not use_z:
                return z
            ends, middle = (3, 2, 1, 0)[i], (3, 0, 2, 1)[i]
            g = ends + here.inner * (middle - ends)
            return g + mirrored * (3 - 2 * g)

        def core_copy(j, i):
            other = here.c_core
            cc = (other + 2) % COLS if j == 0 else other
            k = j * blocks + i
            return remote(
                p_ref.at[place(dest(i), cc)],
                c_buf.at[k],
                c_send.at[k],
                c_recv.at[k],
                here.over_core,
            )

        def y_copy(i):
            return remote(t_buf.at[i], y_buf.at[i], y_send.at[i], y_recv.at[i], here.over_y)

        if use_c:
            for j in range(2):
                for i in range(blocks):
                    core_copy(j, i).start()
            yield
            for i in range(blocks):
                core_copy(0, i).wait_recv()
                far = place(dest(i), here.c_y)

                def add_core(r, step, i=i, far=far):
                    s = pl.ds(r, step)
                    t_buf[i, s, :] = (
                        p_ref[at(far, r, step)].astype(F32) + c_buf[i, s, :].astype(F32)
                    ).astype(BF16)

                chunked(n, add_core)
                y_copy(i).start()
            yield

        def up_copy(i, zz):
            return remote(z_out.at[i], z_up.at[zz], z_send.at[i], up_recv.at[zz], here.up)

        def down_copy(i, zz):
            return remote(z_out.at[i], z_down.at[zz], z_send.at[i], down_recv.at[zz], here.down)

        for i in range(blocks):
            zz = dest(i)
            near = place(zz, c)
            if use_c:
                core_copy(1, i).wait_recv()
                y_copy(i).wait_recv()

            def local(r, step, i=i, near=near):
                total = p_ref[at(near, r, step)].astype(F32)
                if use_c:
                    s = pl.ds(r, step)
                    total = total + c_buf[blocks + i, s, :].astype(F32)
                    total = total + y_buf[i, s, :].astype(F32)
                return total

            if not use_z:

                def store(r, step, local=local):
                    o_ref[pl.ds(r, step), :] = local(r, step).astype(o_ref.dtype)

                chunked(n, store)
            elif i < ROWS - 1:

                def send(copy, buf, first, i=i, zz=zz, local=local):
                    @pl.when(first)
                    def _():
                        def put(r, step):
                            z_out[i, pl.ds(r, step), :] = local(r, step).astype(BF16)

                        chunked(n, put)

                    @pl.when(jnp.logical_not(first))
                    def _():
                        copy(i, zz).wait_recv()

                        def put(r, step):
                            s = pl.ds(r, step)
                            z_out[i, s, :] = (
                                local(r, step) + buf[zz, s, :].astype(F32)
                            ).astype(BF16)

                        chunked(n, put)

                    copy(i, zz).start()

                pl.when(zz > z)(functools.partial(send, up_copy, z_up, z == 0))
                pl.when(zz < z)(functools.partial(send, down_copy, z_down, z == ROWS - 1))
            else:

                def final(bufs, local=local):
                    def put(r, step):
                        s = pl.ds(r, step)
                        total = local(r, step)
                        for buf in bufs:
                            total = total + buf[z, s, :].astype(F32)
                        o_ref[s, :] = total.astype(o_ref.dtype)

                    chunked(n, put)

                pl.when(z > 0)(lambda: up_copy(0, z).wait_recv())
                pl.when(z < ROWS - 1)(lambda: down_copy(0, z).wait_recv())
                pl.when(z == 0)(lambda: final([z_down]))
                pl.when(z == ROWS - 1)(lambda: final([z_up]))
                pl.when(here.inner == 1)(lambda: final([z_up, z_down]))
            yield

        if use_c:
            for i in range(blocks):
                core_copy(0, i).wait_send()
                core_copy(1, i).wait_send()
                y_copy(i).wait_send()
        if use_z:
            for i in range(ROWS - 1):
                up_copy(i, 0).wait_send()

    return Part([p], [jax.ShapeDtypeStruct((n, w), dtype)], scratch, kinds, steps)


def pull_weights(weights, axes, dp):
    outs, shapes = [], []
    for w, axis in zip(weights, axes):
        shape = list(w.shape)
        shape[axis] //= ROWS
        shape[1 - axis] *= ROWS
        outs.append(jax.ShapeDtypeStruct(tuple(shape), w.dtype))
        shapes.append((w.shape[0] // (ROWS if axis == 0 else 1), w.shape[1] // (ROWS if axis else 1)))
    count = len(weights)
    shared = dp == 2
    kinds = {"rows"} | ({"dp"} if shared else set())

    def steps(here, ins, outs, sems):
        send, recv, dp_send, dp_recv = sems

        def source(m, zz, half):
            n, w = shapes[m]
            first = zz * n if axes[m] == 0 else 0
            rows = n // 2 if half else n
            first = first + here.dp * rows if half else first
            cols = slice(None) if axes[m] == 0 else pl.ds(pl.multiple_of(zz * w, w), w)
            return pl.ds(pl.multiple_of(first, rows), rows), cols

        def target(m, zz, half):
            n, w = shapes[m]
            first = zz * n if axes[m] == 1 else 0
            rows = n // 2 if half else n
            first = first + here.dp * rows if half else first
            cols = slice(None) if axes[m] == 1 else pl.ds(pl.multiple_of(zz * w, w), w)
            return pl.ds(pl.multiple_of(first, rows), rows), cols

        def copy(m, zz, landing):
            return remote(
                ins[m].at[source(m, zz, shared)],
                outs[m].at[target(m, landing, shared)],
                send.at[m * ROWS + zz],
                recv.at[m * ROWS + landing],
                here.row(zz),
            )

        def pass_on(m, zz):
            k = m * ROWS + zz
            region = outs[m].at[target(m, zz, True)]
            return remote(region, region, dp_send.at[k], dp_recv.at[k], here.over_dp)

        for m in range(count):
            for _, zz, _ in here.others():
                copy(m, zz, here.z).start()
        for m in range(count):
            from_place, to_place = source(m, here.z, False), target(m, here.z, False)

            def keep(r, step, m=m, from_place=from_place, to_place=to_place):
                outs[m][at(to_place, r, step)] = ins[m][at(from_place, r, step)]

            chunked(shapes[m][0], keep)
        yield
        yield
        yield
        for m in range(count):
            for d in (1, 3, 2):
                zz = (here.z - d + ROWS) % ROWS
                copy(m, here.z, zz).wait_recv()
                if shared:
                    pass_on(m, zz).start()
            yield
        for m in range(count):
            for _, zz, _ in here.others():
                copy(m, zz, here.z).wait_send()
                if shared:
                    pass_on(m, zz).wait_send()
                    pass_on(m, zz).wait_recv()

    sems = [DMA((count * ROWS,))] * 4
    return Part(list(weights), outs, sems, kinds, steps)


def swap_halves_sum(values, axes):
    outs, scratch = [], []
    for v, axis in zip(values, axes):
        n, w = v.shape
        outs.append(jax.ShapeDtypeStruct((n // 2, w), BF16))
        scratch.append(VMEM((n // 2, w), BF16))
    blocks = [ROWS if axis == 1 else 1 for axis in axes]
    total = sum(blocks)
    scratch += [DMA((total,))] * 2

    def steps(here, ins, outs, refs):
        bufs, send, recv = refs[: len(values)], refs[-2], refs[-1]
        work = []
        k = 0
        for m, v in enumerate(values):
            n = v.shape[0] // blocks[m]
            h = n // 2
            for b in range(blocks[m]):
                theirs = pl.ds(pl.multiple_of(b * n + (1 - here.dp) * h, h), h)
                copy = functools.partial(
                    remote,
                    ins[m].at[theirs],
                    bufs[m].at[pl.ds(b * h, h)],
                    send.at[k],
                    recv.at[k],
                    here.over_dp,
                )
                copy().start()
                work.append((m, b, h, n, copy))
                k += 1
        for _ in range(6):
            yield
        for m, b, h, n, copy in work:
            copy().wait_recv()

            def add(r, step, m=m, b=b, h=h, n=n):
                own = pl.ds(pl.multiple_of(b * n + here.dp * h + r, step), step)
                s = pl.ds(pl.multiple_of(b * h + r, step), step)
                outs[m][s, :] = (
                    ins[m][own, :].astype(F32) + bufs[m][s, :].astype(F32)
                ).astype(BF16)

            chunked(h, add)
        for m, b, h, n, copy in work:
            copy().wait_send()

    return Part(list(values), outs, scratch, {"dp"}, steps)


def push_gradients(values, axes, dp):
    shared = dp == 2
    halves = 2 if shared else 1
    outs, shapes = [], []
    for v, axis in zip(values, axes):
        n, w = v.shape
        if axis == 1:
            n = n // ROWS
            outs.append(jax.ShapeDtypeStruct((halves, n, w * ROWS), v.dtype))
        else:
            w = w // ROWS
            outs.append(jax.ShapeDtypeStruct((ROWS, halves, n, w), v.dtype))
        shapes.append((n, w))
    count = len(values)
    kinds = {"rows"} | ({"dp"} if shared else set())

    def steps(here, ins, outs, sems):
        send, recv, dp_send, dp_recv = sems
        half = here.dp if shared else 0

        def block(m, zz):
            n, w = shapes[m]
            if axes[m] == 1:
                return ins[m].at[pl.ds(pl.multiple_of(zz * n, n), n)]
            return ins[m].at[:, pl.ds(pl.multiple_of(zz * w, w), w)]

        def slot(m, zz):
            n, w = shapes[m]
            if axes[m] == 1:
                return outs[m].at[half, :, pl.ds(pl.multiple_of(zz * w, w), w)]
            return outs[m].at[zz, half]

        def copy(m, zz, landing):
            return remote(
                block(m, zz),
                slot(m, landing),
                send.at[m * ROWS + zz],
                recv.at[m * ROWS + landing],
                here.row(zz),
            )

        def pass_on(m, zz):
            k = m * ROWS + zz
            return remote(slot(m, zz), slot(m, zz), dp_send.at[k], dp_recv.at[k], here.over_dp)

        for m in range(count):
            for _, zz, _ in here.others():
                copy(m, zz, here.z).start()
        for m in range(count):

            def keep(r, step, m=m):
                s = pl.ds(r, step)
                slot(m, here.z)[s, :] = block(m, here.z)[s, :]

            chunked(shapes[m][0], keep)
            if shared:
                pass_on(m, here.z).start()
        for _ in range(4):
            yield
        for m in range(count):
            for d in (1, 3, 2):
                zz = (here.z - d + ROWS) % ROWS
                copy(m, here.z, zz).wait_recv()
                if shared:
                    pass_on(m, zz).start()
            yield
        for m in range(count):
            for _, zz, _ in here.others():
                copy(m, zz, here.z).wait_send()
            if shared:
                for zz in range(ROWS):
                    pass_on(m, zz).wait_send()
                    remote(
                        slot(m, zz), slot(m, zz), dp_send.at[0], dp_recv.at[m * ROWS + zz], here.over_dp
                    ).wait_recv()

    sems = [DMA((count * ROWS,))] * 4
    return Part(list(values), outs, sems, kinds, steps)


def swap(values):
    outs = [jax.ShapeDtypeStruct(v.shape, v.dtype) for v in values]

    def steps(here, ins, outs, sems):
        copies = [
            remote(i, o, sems[0].at[k], sems[1].at[k], here.over_dp)
            for k, (i, o) in enumerate(zip(ins, outs))
        ]
        for copy in copies:
            copy.start()
        for _ in range(20):
            yield
        for copy in copies:
            copy.wait()

    return Part(list(values), outs, [DMA((len(values),))] * 2, {"dp"}, steps)


def sum_gains(vector, n_dp):
    shape = vector.shape

    def steps(here, ins, outs, refs):
        (v_ref,), (o_ref,) = ins, outs
        buf, part, groups, send, recv, dp_send, dp_recv = refs
        me = here.z * COLS + here.c
        for k, zz, cc in here.peers():
            remote(v_ref, buf.at[me], send.at[k], recv.at[me], (here.dp, zz, cc)).start()
        buf[me] = v_ref[...]
        yield
        for k, zz, cc in here.peers():
            source = zz * COLS + cc
            copy = remote(
                v_ref, buf.at[source], send.at[k], recv.at[source], (here.dp, zz, cc)
            )
            copy.wait_send()
            copy.wait_recv()
        for zz in range(ROWS):
            part[zz] = buf[zz * COLS] + buf[zz * COLS + 1] + buf[zz * COLS + 2] + buf[zz * COLS + 3]
        groups[here.dp] = part[...]
        for d in range(1, n_dp):
            remote(
                part, groups.at[here.dp], dp_send.at[d], dp_recv.at[here.dp], here.group(d)
            ).start()
        yield
        for d in range(1, n_dp):
            source = (here.dp + d) % n_dp
            copy = remote(
                part, groups.at[source], dp_send.at[d], dp_recv.at[source], here.group(d)
            )
            copy.wait_send()
            copy.wait_recv()
        total = groups[0]
        for d in range(1, n_dp):
            total = total + groups[d]
        o_ref[...] = total

    scratch = [
        VMEM((ROWS * COLS,) + shape, F32),
        VMEM((ROWS,) + shape, F32),
        VMEM((n_dp, ROWS) + shape, F32),
        DMA((ROWS * COLS,)),
        DMA((ROWS * COLS,)),
        DMA((n_dp,)),
        DMA((n_dp,)),
    ]
    outs = [jax.ShapeDtypeStruct((ROWS,) + shape, F32)]
    return Part([vector], outs, scratch, {"plane", "dp"}, steps)


class Plan:
    def __init__(self):
        self.specs, self.kinds = [], set()

    def add(self, part):
        first = len(self.specs)
        self.specs += part.scratch
        self.kinds |= part.kinds
        return part, first

    def buffer(self, shape, dtype):
        self.specs.append(VMEM(shape, dtype))
        return len(self.specs) - 1

    def bind(self, here, refs):
        self.here, self.refs = here, refs

    def __getitem__(self, handle):
        return self.refs[handle]

    def start(self, handle, ins, outs):
        part, first = handle
        steps = part.steps(self.here, ins, outs, self.refs[first : first + len(part.scratch)])
        next(steps, None)
        return steps


def advance(steps, count=1):
    for _ in range(count):
        next(steps, None)


def finish(steps):
    for _ in steps:
        pass


def like(shape, dtype):
    return jax.ShapeDtypeStruct(shape, dtype)


def planned(n_dp, call, name, plan, args, outs, body):
    ins, out_list = vars(args), vars(outs)

    def kernel(*refs):
        here = Here(n_dp)
        i = SimpleNamespace(**dict(zip(ins, refs)))
        o = SimpleNamespace(**dict(zip(out_list, refs[len(ins) :])))
        plan.bind(here, refs[len(ins) + len(out_list) :])
        meet(here, plan.kinds)
        body(i, o)

    vmem = pl.BlockSpec(memory_space=VMEM)
    results = pl.pallas_call(
        kernel,
        out_shape=list(out_list.values()),
        in_specs=[vmem] * len(ins),
        out_specs=[vmem] * len(out_list),
        scratch_shapes=plan.specs,
        compiler_params=pltpu.CompilerParams(
            collective_id=call, has_side_effects=True, vmem_limit_bytes=63 << 20
        ),
        name=name,
    )(*ins.values())
    return SimpleNamespace(**dict(zip(out_list, results)))


def rows_times(o_ref, a_ref, terms, block=256):
    def body(i, _):
        s = pl.ds(pl.multiple_of(i * block, block), block)
        total = None
        for columns, b_ref, flipped in terms:
            term = dot(a_ref[s, columns], b_ref[...], flipped)
            total = term if total is None else total + term
        o_ref[s, :] = total.astype(o_ref.dtype)
        return 0

    lax.fori_loop(0, a_ref.shape[0] // block, body, 0)


def columns_times(o_ref, a_ref, b_ref, height=256, width=512):
    across = b_ref.shape[1] // width

    def body(i, _):
        m = pl.ds(pl.multiple_of(i // across * height, height), height)
        n = pl.ds(pl.multiple_of(i % across * width, width), width)
        o_ref[m, n] = weight_term(a_ref[:, m], b_ref[:, n]).astype(o_ref.dtype)
        return 0

    lax.fori_loop(0, a_ref.shape[1] // height * across, body, 0)


ALL = slice(None)


def swapped(field):
    return pltpu.roll(field, HEAD_SIZE // 2, 1)


def lane_major(column):
    return jnp.transpose(jnp.broadcast_to(column, (column.shape[0], HEAD_SIZE)))[:8]


def token_major(row):
    return jnp.transpose(jnp.broadcast_to(row, (HEAD_SIZE, row.shape[1])))


def head_at(ref, h):
    return ref[:, pl.ds(h * HEAD_SIZE, HEAD_SIZE)]


def make_tables(seg_ref, inverse_ref, sign_ref, o):
    row = seg_ref[...].astype(F32)
    n = row.shape[1]
    column = token_major(row)[:, 0:1]
    query = lax.broadcasted_iota(jnp.int32, (n, n), 0)
    key = lax.broadcasted_iota(jnp.int32, (n, n), 1)
    allowed = (column == row) & (key <= query)
    o.bias[...] = jnp.where(allowed, 0.0, -1e30)
    position = jnp.sum(jnp.where(allowed, 1.0, 0.0), axis=-1, keepdims=True) - 1.0
    angle = position * inverse_ref[...]
    o.cosine[...] = jnp.cos(angle)
    o.sine[...] = jnp.sin(angle) * sign_ref[...]


def attention_forward(i, o):
    heads, groups = o.q.shape[1] // HEAD_SIZE, o.k.shape[1] // HEAD_SIZE
    each = heads // groups
    scale = HEAD_SIZE ** (-0.5)
    lane = lax.broadcasted_iota(jnp.int32, o.lse.shape, 1)

    def turned(at_head, gain_ref):
        raw = head_at(o.joint, at_head)
        norm = lax.rsqrt(jnp.mean(raw * raw, axis=-1, keepdims=True) + EPSILON)
        field = raw * norm * gain_ref[...]
        return (field * o.cosine[...] + swapped(field) * o.sine[...]).astype(BF16)

    for g in range(groups):
        at_head = pl.ds(g * HEAD_SIZE, HEAD_SIZE)
        o.k[:, at_head] = turned(heads + g, i.key_gain)
        o.v[:, at_head] = head_at(o.joint, heads + groups + g).astype(BF16)
        for h in range(g * each, (g + 1) * each):
            query = turned(h, i.query_gain)
            o.q[:, pl.ds(h * HEAD_SIZE, HEAD_SIZE)] = query
            scores = dot(query, o.k[:, at_head], True) * scale + o.bias[...]
            top = jnp.max(scores, axis=-1, keepdims=True)
            weights = jnp.exp(scores - top)
            total = jnp.sum(weights, axis=-1, keepdims=True)
            probs = (weights / total).astype(BF16)
            o.mixed[:, pl.ds(h * HEAD_SIZE, HEAD_SIZE)] = dot(probs, o.v[:, at_head]).astype(BF16)
            log_total = jnp.broadcast_to(top + jnp.log(total), o.lse.shape)
            if h == 0:
                o.lse[...] = log_total
            else:
                o.lse[...] = jnp.where(lane == h, log_total, o.lse[...])
            yield


def forward(n_dp, call, a):
    length, feats = a.layer_input.shape
    query_width, key_width = a.w_query.shape[1], a.key_matrix.shape[1]
    wide = query_width + 2 * key_width
    tokens = length * COLS
    units = a.w_gate.shape[1] // ROWS
    plan = Plan()
    in_gather = plan.add(gather(a.layer_input, False, True))
    joint_sum = plan.add(scatter_sum(like((tokens, wide), BF16), True, False))
    in_stat = plan.add(send_stats(like((ROWS, 8, length), F32), row_stats))
    cot_gather = plan.add(gather(a.cotangent, True, True))
    mix_gather = plan.add(gather(like((length, query_width), BF16), True, False))
    out_sum = plan.add(scatter_sum(like((tokens, feats), BF16), False, True))
    mid_gather = plan.add(gather(like((length, feats), BF16), True, True, like((8, length), F32)))
    pulls = [
        pull_weights([a.w_down], [0], n_dp),
        pull_weights([a.w_gate], [1], n_dp),
        pull_weights([a.w_up], [1], n_dp),
    ]
    pull_low, pull_gate, pull_up = [plan.add(p) for p in pulls]
    in_rows = plan.buffer((tokens, feats), BF16)
    stats = plan.buffer((ROWS, 8, length), F32)
    got_stats = plan.buffer((ROWS, 8, length), F32)
    mid_stats = plan.buffer((ROWS * COLS, 8, length), F32)
    own_stat = plan.buffer((8, length), F32)
    p_joint = plan.buffer((tokens, wide), BF16)
    p_out = plan.buffer((tokens, feats), BF16)
    attn_out = plan.buffer((length, feats), F32)
    gained = plan.buffer((length, feats), BF16)
    outs = SimpleNamespace(
        in_gained=like((tokens, feats), BF16),
        joint=like((length, wide), F32),
        scale_in=like((length, HEAD_SIZE), F32),
        bias=like((length, length), F32),
        cosine=like((length, HEAD_SIZE), F32),
        sine=like((length, HEAD_SIZE), F32),
        q=like((length, query_width), BF16),
        k=like((length, key_width), BF16),
        v=like((length, key_width), BF16),
        mixed=like((length, query_width), BF16),
        lse=like((length, HEAD_SIZE), F32),
        mix_rows=like((tokens, query_width), BF16),
        hidden=like((length, feats), F32),
        mid_rows=like((tokens, MODEL_WIDTH), BF16),
        scale_mid=like((tokens, HEAD_SIZE), F32),
        cot_rows=like((tokens, MODEL_WIDTH), BF16),
        w_low=pulls[0].outs[0],
        w_gate_all=pulls[1].outs[0],
        w_up_all=pulls[2].outs[0],
        grad_active=like((tokens, units), F32),
    )

    def body(i, o):
        first = plan.start(in_gather, [i.layer_input], [plan[in_rows]])
        low = plan.start(pull_low, [i.w_down], [o.w_low])
        make_tables(i.segment, i.inverse, i.sign, o)
        finish(first)

        def normed(b, _):
            s = pl.ds(pl.multiple_of(b * length, length), length)
            field = plan[in_rows][s, :].astype(F32)
            o.in_gained[s, :] = (field * i.attn_gain[...]).astype(BF16)
            plan[stats][b] = lane_major(jnp.sum(field * field, axis=-1, keepdims=True))
            for columns, w_ref in (
                (pl.ds(0, query_width), i.w_query),
                (pl.ds(query_width, key_width), i.key_matrix),
                (pl.ds(query_width + key_width, key_width), i.value_matrix),
            ):
                plan[p_joint][s, columns] = dot(o.in_gained[s, :], w_ref[...]).astype(BF16)
            return 0

        lax.fori_loop(0, COLS, normed, 0)
        total = plan.start(joint_sum, [plan[p_joint]], [o.joint])
        stat = plan.start(in_stat, [plan[stats]], [plan[got_stats]])
        finish(total)
        finish(stat)
        cot = plan.start(cot_gather, [i.cotangent], [o.cot_rows])
        summed = plan[got_stats][0] + plan[got_stats][1] + plan[got_stats][2] + plan[got_stats][3]
        o.scale_in[...] = lax.rsqrt(token_major(summed[0:1]) / MODEL_WIDTH + EPSILON)

        def scaled(r, step):
            s = pl.ds(r, step)
            o.joint[s, :] = o.joint[s, :] * o.scale_in[s, 0:1]

        chunked(length, scaled)
        for _ in attention_forward(i, o):
            pass
        mix = plan.start(mix_gather, [o.mixed], [o.mix_rows])
        advance(cot, 2)
        advance(mix)
        advance(cot, 2)
        advance(mix)
        advance(cot, 2)
        finish(mix)
        gate = plan.start(pull_gate, [i.w_gate], [o.w_gate_all])
        rows_times(plan[p_out], o.mix_rows, [(ALL, i.w_output, False)])
        out = plan.start(out_sum, [plan[p_out]], [plan[attn_out]])
        finish(cot)
        finish(out)
        finish_low = low

        def add(r, step):
            s = pl.ds(r, step)
            field = i.layer_input[s, :].astype(F32) + plan[attn_out][s, :]
            o.hidden[s, :] = field
            plan[gained][s, :] = (field * i.mlp_gain[...]).astype(BF16)

        chunked(length, add)
        plan[own_stat][...] = lane_major(
            jnp.sum(o.hidden[...] * o.hidden[...], axis=-1, keepdims=True)
        )
        mid = plan.start(
            mid_gather, [plan[gained], plan[own_stat]], [o.mid_rows, plan[mid_stats]]
        )
        up = plan.start(pull_up, [i.w_up], [o.w_up_all])
        finish(finish_low)
        advance(mid, 2)
        rows_times(o.grad_active, o.cot_rows, [(ALL, o.w_low, True)])
        advance(mid, 2)
        advance(gate, 4)
        finish(mid)
        for b in range(COLS):
            summed = plan[mid_stats][b]
            for zz in range(1, ROWS):
                summed = summed + plan[mid_stats][zz * COLS + b]
            o.scale_mid[pl.ds(b * length, length), :] = lax.rsqrt(
                token_major(summed[0:1]) / MODEL_WIDTH + EPSILON
            )
        finish(gate)
        finish(up)

    return planned(n_dp, call, "forward", plan, a, outs, body)


def attention_back(i, grad_mixed, gj_ref, inner_ref, gains_ref, dk_ref, dv_ref):
    heads, groups = i.q.shape[1] // HEAD_SIZE, i.k.shape[1] // HEAD_SIZE
    each = heads // groups
    scale = HEAD_SIZE ** (-0.5)
    cosine, sine = i.cosine[...], i.sine[...]
    scale_in = i.scale_in[:, 0:1]
    inner = jnp.zeros((i.q.shape[0], HEAD_SIZE), F32)

    def norm_back(grad_rot, at_head, gain):
        grad = grad_rot * cosine - swapped(grad_rot) * sine
        raw = head_at(i.joint, at_head)
        norm = lax.rsqrt(jnp.mean(raw * raw, axis=-1, keepdims=True) + EPSILON)
        unit = raw * norm
        u = grad * gain
        back = norm * (u - unit * jnp.mean(u * unit, axis=-1, keepdims=True))
        out = (back * scale_in).astype(BF16)
        gj_ref[:, pl.ds(at_head * HEAD_SIZE, HEAD_SIZE)] = out
        return out.astype(F32) * raw, jnp.sum(grad * unit, axis=0, keepdims=True)

    gain_q = jnp.zeros((1, HEAD_SIZE), F32)
    gain_k = jnp.zeros((1, HEAD_SIZE), F32)
    for g in range(groups):
        key, value = head_at(i.k, g), head_at(i.v, g)
        for r in range(each):
            h = g * each + r
            query, grad = head_at(i.q, h), head_at(grad_mixed, h)
            scores = dot(query, key, True) * scale + i.bias[...]
            probs = jnp.exp(scores - i.lse[:, h : h + 1])
            term_v = weight_term(probs.astype(BF16), grad)
            delta = jnp.sum(
                grad.astype(F32) * head_at(i.mixed, h).astype(F32), axis=-1, keepdims=True
            )
            grad_scores = (probs * (dot(grad, value, True) - delta)).astype(BF16)
            term_k = weight_term(grad_scores, query) * scale
            if r == 0:
                dv_ref[...] = term_v
                dk_ref[...] = term_k
            else:
                dv_ref[...] += term_v
                dk_ref[...] += term_k
            term, gain = norm_back(dot(grad_scores, key) * scale, h, i.query_gain[...])
            inner = inner + term
            gain_q = gain_q + gain
        term, gain = norm_back(dk_ref[...], heads + g, i.key_gain[...])
        inner = inner + term
        gain_k = gain_k + gain
        at_head = heads + groups + g
        out = (dv_ref[...] * scale_in).astype(BF16)
        gj_ref[:, pl.ds(at_head * HEAD_SIZE, HEAD_SIZE)] = out
        inner = inner + out.astype(F32) * head_at(i.joint, at_head)
    gains_ref[8:9, :] = gain_q
    gains_ref[9:10, :] = gain_k
    inner_ref[0] = lane_major(jnp.sum(inner, axis=-1, keepdims=True) * scale_in)


def backward(n_dp, call, a):
    two = n_dp == 2
    length, feats = a.grad_attn.shape
    query_width, key_width = a.w_query.shape[1], a.key_matrix.shape[1]
    wide = query_width + 2 * key_width
    tokens = length * COLS
    plan = Plan()
    attn_gather = plan.add(gather(a.grad_attn, False, True))
    mixed_sum = plan.add(scatter_sum(like((tokens, feats), BF16), True, False, BF16))
    joint_gather = plan.add(gather(like((length, wide), BF16), True, False))
    in_sum = plan.add(scatter_sum(like((tokens, feats), BF16), False, True))
    in_stat = plan.add(send_stats(like((1, 8, length), F32), owner_stats))
    block_sum = plan.add(scatter_sum(like((tokens, MODEL_WIDTH), BF16), True, True))
    n, w = a.grad_gate.shape
    half = like((n // 2 if two else n, w), BF16)
    if two:
        gate_half = plan.add(swap_halves_sum([a.grad_gate], [1]))
        up_half = plan.add(swap_halves_sum([a.grad_up], [1]))
        gate_sum = plan.buffer(half.shape, BF16)
        up_sum = plan.buffer(half.shape, BF16)
    pushes = [
        push_gradients([half], [1], n_dp),
        push_gradients([half], [1], n_dp),
        push_gradients([a.grad_low], [0], n_dp),
    ]
    gate_push, up_push, low_push = [plan.add(p) for p in pushes]
    gain_sum = plan.add(sum_gains(like((16, HEAD_SIZE), F32), n_dp))
    d_output, d_joint = like((feats, feats), BF16), like((feats, wide), BF16)
    if two:
        output_swap = plan.add(swap([d_output]))
        joint_swap = plan.add(swap([d_joint]))
    attn_rows = plan.buffer((tokens, feats), BF16)
    p_mixed = plan.buffer((tokens, feats), BF16)
    grad_mixed = plan.buffer((length, feats), BF16)
    joint_in = plan.buffer((length, wide), BF16)
    joint_rows = plan.buffer((tokens, wide), BF16)
    p_in = plan.buffer((tokens, feats), BF16)
    p_block = plan.buffer((tokens, MODEL_WIDTH), BF16)
    inner = plan.buffer((1, 8, length), F32)
    gain_rows = plan.buffer((16, HEAD_SIZE), F32)
    dk, dv = [plan.buffer((length, HEAD_SIZE), F32) for _ in range(2)]
    outs = SimpleNamespace(
        grad_in=like((length, feats), F32),
        in_inners=like((COLS, 8, length), F32),
        block=like((length, feats), F32),
        grad_gate=pushes[0].outs[0],
        grad_up=pushes[1].outs[0],
        grad_low=pushes[2].outs[0],
        gains=like((ROWS, 16, HEAD_SIZE), F32),
        d_output=d_output,
        d_joint=d_joint,
    )
    if two:
        outs.d_output_other, outs.d_joint_other = d_output, d_joint

    def body(i, o):
        attn = plan.start(attn_gather, [i.grad_attn], [plan[attn_rows]])
        low = plan.start(low_push, [i.grad_low], [o.grad_low])
        if two:
            halves = [
                plan.start(gate_half, [i.grad_gate], [plan[gate_sum]]),
                plan.start(up_half, [i.grad_up], [plan[up_sum]]),
            ]
        rows_times(plan[p_block], i.active, [(ALL, i.w_low, False)])
        finish(attn)
        rows_times(plan[p_mixed], plan[attn_rows], [(ALL, i.w_output, True)])
        mixed = plan.start(mixed_sum, [plan[p_mixed]], [plan[grad_mixed]])
        block = plan.start(block_sum, [plan[p_block]], [o.block])
        columns_times(o.d_output, i.mix_rows, plan[attn_rows])
        if two:
            swap_output = plan.start(output_swap, [o.d_output], [o.d_output_other])
        finish(mixed)
        if two:
            finish(halves[0])
        gate = plan.start(gate_push, [plan[gate_sum] if two else i.grad_gate], [o.grad_gate])
        plan[gain_rows][...] = i.gain_mid[...]
        attention_back(
            i,
            plan[grad_mixed],
            plan[joint_in],
            plan[inner],
            plan[gain_rows],
            plan[dk],
            plan[dv],
        )
        joint = plan.start(joint_gather, [plan[joint_in]], [plan[joint_rows]])
        stat = plan.start(in_stat, [plan[inner]], [o.in_inners])
        finish(low)
        advance(block)
        if two:
            finish(halves[1])
        finish(joint)
        up = plan.start(up_push, [plan[up_sum] if two else i.grad_up], [o.grad_up])
        columns_times(o.d_joint, i.in_gained, plan[joint_rows])
        if two:
            swap_joint = plan.start(joint_swap, [o.d_joint], [o.d_joint_other])
        rows_times(
            plan[p_in],
            plan[joint_rows],
            [
                (pl.ds(0, query_width), i.w_query, True),
                (pl.ds(query_width, key_width), i.key_matrix, True),
                (pl.ds(query_width + key_width, key_width), i.value_matrix, True),
            ],
        )
        grad_in = plan.start(in_sum, [plan[p_in]], [o.grad_in])
        finish(gate)
        finish(grad_in)
        total = jnp.sum(o.grad_in[...] * i.layer_input[...].astype(F32), axis=0, keepdims=True)
        for k in range(feats // HEAD_SIZE):
            plan[gain_rows][k : k + 1, :] = total[:, k * HEAD_SIZE : (k + 1) * HEAD_SIZE]
        gains = plan.start(gain_sum, [plan[gain_rows]], [o.gains])
        finish(block)
        finish(gains)
        finish(stat)
        finish(up)
        if two:
            finish(swap_output)
            finish(swap_joint)

    return planned(n_dp, call, "backward", plan, a, outs, body)


def silu_parts(gate):
    sigma = jax.nn.sigmoid(gate)
    return (gate * sigma, sigma * (1.0 + gate * (1.0 - sigma)))


def dot(left, right, flipped=False):
    return lax.dot_general(
        left, right, (((1,), (1 if flipped else 0,)), ((), ())), preferred_element_type=F32
    )


def weight_term(left, right):
    return lax.dot_general(left, right, (((0,), (0,)), ((), ())), preferred_element_type=F32)


def per_device(
    dp,
    layer_input,
    cotangent,
    w_query,
    key_matrix,
    value_matrix,
    w_output,
    w_gate,
    w_up,
    w_down,
    attn_gain,
    mlp_gain,
    query_gain,
    key_gain,
    segment_ids,
):
    length, feats = layer_input.shape
    query_width, key_width = w_query.shape[1], key_matrix.shape[1]
    ff_local = w_gate.shape[1]
    two = dp == 2
    half = jnp.arange(HEAD_SIZE // 2, dtype=F32)
    inverse = jnp.power(THETA, -(half * (2.0 / HEAD_SIZE)))
    ones = jnp.ones_like(half)
    f = forward(
        dp,
        0,
        SimpleNamespace(
            layer_input=layer_input,
            cotangent=cotangent,
            w_query=w_query,
            key_matrix=key_matrix,
            value_matrix=value_matrix,
            w_output=w_output,
            w_gate=w_gate,
            w_up=w_up,
            w_down=w_down,
            attn_gain=attn_gain[None],
            mlp_gain=mlp_gain[None],
            query_gain=query_gain[None],
            key_gain=key_gain[None],
            segment=segment_ids,
            inverse=jnp.concatenate([inverse, inverse])[None],
            sign=jnp.concatenate([-ones, ones])[None],
        ),
    )
    scale_mid = f.scale_mid[:, 0:1]
    gate = dot(f.mid_rows, f.w_gate_all) * scale_mid
    upward = dot(f.mid_rows, f.w_up_all) * scale_mid
    silu, slope = silu_parts(gate)
    active = (silu * upward).astype(BF16)
    grad_gated = f.grad_active * scale_mid
    grad_gate_in = (grad_gated * upward * slope).astype(BF16)
    grad_up_in = (grad_gated * silu).astype(BF16)
    mid_inner = jnp.sum(
        grad_gate_in.astype(F32) * gate + grad_up_in.astype(F32) * upward, axis=-1, keepdims=True
    )
    grad_low = weight_term(active, f.cot_rows).astype(BF16)
    grad_mid_part = dot(grad_gate_in, f.w_gate_all, True) + dot(grad_up_in, f.w_up_all, True)
    parts = [
        scatter_sum(grad_mid_part.astype(BF16), True, True),
        send_stats((mid_inner * scale_mid).reshape(COLS, 2, HEAD_SIZE), plane_stats),
    ]
    if two:
        parts.append(swap_halves_sum([grad_low], [0]))
    else:
        grad_low = lax.psum(grad_low, "dp")
    (grad_mid,), (mid_inners,), *low = run_parts(dp, 1, *parts)
    if two:
        ((grad_low,),) = low
    grad_gate = weight_term(f.mid_rows, grad_gate_in).astype(BF16)
    grad_up = weight_term(f.mid_rows, grad_up_in).astype(BF16)
    mid_coef = jnp.sum(mid_inners, axis=0).reshape(length, 1) / MODEL_WIDTH
    gain_mid = jnp.sum(grad_mid * f.hidden, axis=0)
    grad_hidden = cotangent.astype(F32) + grad_mid * mlp_gain - f.hidden * mid_coef
    grad_attn = grad_hidden.astype(BF16)
    if not two:
        grad_gate, grad_up = lax.psum(grad_gate, "dp"), lax.psum(grad_up, "dp")
    b = backward(
        dp,
        2,
        SimpleNamespace(
            grad_attn=grad_attn,
            w_output=w_output,
            w_query=w_query,
            key_matrix=key_matrix,
            value_matrix=value_matrix,
            q=f.q,
            k=f.k,
            v=f.v,
            mixed=f.mixed,
            lse=f.lse,
            bias=f.bias,
            cosine=f.cosine,
            sine=f.sine,
            joint=f.joint,
            scale_in=f.scale_in,
            query_gain=query_gain[None],
            key_gain=key_gain[None],
            mix_rows=f.mix_rows,
            in_gained=f.in_gained,
            active=active,
            w_low=f.w_low,
            grad_gate=grad_gate,
            grad_up=grad_up,
            grad_low=grad_low,
            gain_mid=jnp.pad(gain_mid.reshape(-1, HEAD_SIZE), ((4, 8), (0, 0))),
            layer_input=layer_input,
        ),
    )
    if two:
        grad_output = b.d_output.astype(F32) + b.d_output_other.astype(F32)
        grad_joint = b.d_joint.astype(F32) + b.d_joint_other.astype(F32)
    else:
        grad_output, grad_joint = lax.psum((b.d_output, b.d_joint), "dp")
        grad_output, grad_joint = grad_output.astype(F32), grad_joint.astype(F32)
    in_coef = jnp.sum(b.in_inners[:, 0], axis=0).reshape(length, 1) / MODEL_WIDTH
    input_grad = grad_hidden + b.grad_in * attn_gain - layer_input.astype(F32) * in_coef
    return (
        (f.hidden + b.block).astype(BF16),
        input_grad,
        grad_joint[:, :query_width],
        grad_joint[:, query_width : query_width + key_width],
        grad_joint[:, query_width + key_width :],
        grad_output,
        b.grad_gate.reshape(feats, ff_local).astype(F32),
        b.grad_up.reshape(feats, ff_local).astype(F32),
        b.grad_low.reshape(ff_local, feats).astype(F32),
        b.gains[:, 0:4].reshape(MODEL_WIDTH),
        b.gains[:, 4:8].reshape(MODEL_WIDTH),
        jnp.sum(b.gains[:, 8], axis=0),
        jnp.sum(b.gains[:, 9], axis=0),
    )


def solution(mesh):
    tokens, weights, flipped = P(("dp", "col"), "row"), P("row", "col"), P("col", "row")
    features, copied = P("row"), P()
    return jax.shard_map(
        functools.partial(per_device, mesh.shape["dp"]),
        mesh=mesh,
        in_specs=(
            (tokens, tokens)
            + (weights,) * 3
            + (flipped, weights, weights, flipped)
            + (features, features, copied, copied, P(("dp", "row"), None))
        ),
        out_specs=(tokens, tokens)
        + (weights,) * 3
        + (flipped, weights, weights, flipped)
        + (copied,) * 4,
        check_vma=False,
    )
```

time: 1180 us -> 457 us (0.39)
  waiting for transfers between devices: 929 us -> 0 us
  Pallas kernels: 0 us -> 405 us
  blocking collectives: 87.3 us -> 0 us
  matrix products: 69.7 us -> 28.8 us
  local copies, waits for them, and re-layouts: 37.7 us -> 6.22 us
  other arithmetic: 37.9 us -> 15.5 us
  between operations: 14.6 us -> 0.86 us
    reduce_scatter x8 -> x0, waiting for transfers between devices: 498 us -> none  [the longest x4 431 us: row_product(): lax.psum_scatter(matrix_result(gathered, weight, flipped), 'row', scatter...]
    pallas_call x0 -> x3, Pallas kernels: none -> 405 us  [the longest x2 369 us: planned(): pl.pallas_call(kernel, out_shape=list(out_list.values()), in_specs=[vmem]...]
    all_gather x8 -> x0, waiting for transfers between devices: 291 us -> none  [the longest x4 251 us: gather_rows(): return lax.all_gather(piece, 'row', axis=0, tiled=True)]
    psum x1 -> x0, waiting for transfers between devices: 138 us -> none  [per_device(): lax.psum(grad_joint.astype(jnp.bfloat16), 'dp').astype(jnp.float32)]
    psum x5 -> x0, blocking collectives: 87.3 us -> none  [the longest x4 49.7 us: row_stats(): return lax.psum(partial_value, 'row')]
    dot_general x14 -> x4, matrix products: 53 us -> 16.1 us  [dot(): lax.dot_general(left, right, (((1,), (1 if flipped else 0,)), ((), ())),...]
  transfers between devices with their start and end apart: 17 -> 0, of which waited for: 16 -> 0; matrix products, arithmetic and copies ran while one was open for 5% -> 0% of each run, Pallas kernels for 0% -> 0%
where the time goes in v1:
time: 457 us
  Pallas kernels  405 us (89%)
  matrix products  28.8 us (6%)
  other arithmetic  15.5 us (3%)
  local copies, waits for them, and re-layouts  6.22 us (1%)
    pallas_call x2, Pallas kernels, planned(): pl.pallas_call(kernel, out_shape=list(out_list.values()), in_specs=[vmem]...  369 us
    pallas_call x1, Pallas kernels, run_parts(): pl.pallas_call(kernel, out_shape=[o for p in parts for o in p.outs], in_s...  36.6 us
    dot_general x4, matrix products, dot(): lax.dot_general(left, right, (((1,), (1 if flipped else 0,)), ((), ())),...  16.1 us
    dot_general x3, matrix products, weight_term(): lax.dot_general(left, right, (((0,), (0,)), ((), ())), preferred_element_...  12.7 us

profile of v1, /device:TPU:0, one launch (start us, length us, event | category | flops | bytes accessed | tf_op | source)
XLA Modules:
  0.0 456.6 jit_solution(14548378947215549463)
XLA Ops:
  1.2 182.3 %forward.1 = (bf16[1024,512]{1,0:T(8,128)(2,1)}, f32[256,1024]{1,0:T(8,128)}, f32[256,128]{1,0:T(8,128)}, f32[256,256]{1,0:T(8,128)}, f32[256,128]{1,0:T(8,128)}...) custom-call(bf16[256,512]{1,0:T(8,128)(2,1)} %refs_25_.1, ...), custom_call_target="tpu_custom_call" | custom-call | tf_op jit(solution)/shard_map/forward/pallas_call | solution.py:859
  183.6 1.2 slice_reduce_fusion
  184.9 5.1 %convolution_multiply_fusion = f32[1024,384]{1,0:T(8,128)S(1)} fusion(bf16[1024,2048]{1,0:T(8,128)(2,1)} %get-tuple-element.50, bf16[2048,384]{1,0:T(8,128)(2,1)} %get-tuple-element.52, f32[1024]{0:T(1024)S(1)} %slice_reduce_fusion), kind=kOutput, calls=%fused_computation.14 | convolution fusion | flops 1611005952 | bytes 7344128 | tf_op jit(solution)/shard_map/dot_general | solution.py:1282
  190.0 4.0 add_reduce_fusion
  194.1 3.0 convolution_convert_fusion.2.refs_2_
  197.3 0.8 multiply_reduce_fusion.1
  198.1 6.1 %convolution_convert_fusion.refs_22_ = bf16[2048,384]{1,0:T(8,128)(2,1)} fusion(bf16[1024,2048]{1,0:T(8,128)(2,1)} %get-tuple-element.50, bf16[1024,384]{1,0:T(8,128)(2,1)} %get-tuple-element.84), kind=kOutput, calls=%fused_computation.1 | convolution fusion | flops 1611399168 | bytes 6553600 | tf_op jit(solution)/shard_map/dot_general | solution.py:1288
  204.2 3.6 convolution_convert_fusion.1.refs_21_
  207.8 2.6 fusion.4
  210.4 4.3 add_convert_fusion.refs_0_
  214.8 36.6 %stage_1.1 = (f32[256,512]{1,0:T(8,128)}, f32[16,2,128]{2,1,0:T(2,128)}, bf16[192,2048]{1,0:T(8,128)(2,1)}) custom-call(bf16[1024,2048]{1,0:T(8,128)(2,1)} %add_convert_fusion.refs_0_, f32[4,2,128]{2,1,0:T(2,128)} %bitcast.37, bf16[384,2048]{1,0:T(8,128)(2,1)} %convolution_convert_fusion.2.refs_2_), custom_call_target="tpu_custom_call" | custom-call | tf_op jit(solution)/shard_map/stage_1/pallas_call | solution.py:123
  251.3 0.7 reduce_sum.55
  252.1 1.9 multiply_reduce_fusion
  254.0 0.6 pad.4.refs_24_
  254.6 186.3 %backward.1 = (f32[256,512]{1,0:T(8,128)}, f32[4,8,256]{2,1,0:T(8,128)}, f32[256,512]{1,0:T(8,128)}, bf16[2,256,1536]{2,1,0:T(8,128)(2,1)}, bf16[2,256,1536]{2,1...) custom-call(bf16[256,512]{1,0:T(8,128)(2,1)} %get-tuple-element.90.r, ...), custom_call_target="tpu_custom_call" | custom-call | tf_op jit(solution)/shard_map/backward/pallas_call | solution.py:859
  440.9 0.8 slice_reduce_fusion.1
  441.8 2.7 multiply_subtract_fusion
  445.6 1.1 convert_add_fusion.1
  447.1 1.1 slice.36
  448.2 1.0 fusion.2
  449.2 0.7 copy-done.8
  450.0 2.2 bitcast_convert_fusion
  452.2 0.6 copy-done.5
  452.8 3.8 bitcast_convert_fusion.1
  (50 shorter events, 2.4 us)
Async XLA Ops:
  184.8 5.2 %copy-start.6 = (bf16[2048,384]{1,0:T(8,128)(2,1)S(1)}, bf16[2048,384]{1,0:T(8,128)(2,1)}, u32[]{:S(2)}) copy-start(bf16[2048,384]{1,0:T(8,128)(2,1)} %get-tuple-element.51) | copy-start | bytes 4718596
  184.8 5.2 %copy-start.18 = (bf16[1024,2048]{1,0:T(8,128)(2,1)S(1)}, bf16[1024,2048]{1,0:T(8,128)(2,1)}, u32[]{:S(2)}) copy-start(bf16[1024,2048]{1,0:T(8,128)(2,1)} %get-tuple-element.50) | copy-start | bytes 12582916
  184.8 5.2 %copy-start.21 = (f32[1024,384]{1,0:T(8,128)S(1)}, f32[1024,384]{1,0:T(8,128)}, u32[]{:S(2)}) copy-start(f32[1024,384]{1,0:T(8,128)} %get-tuple-element.48) | copy-start | bytes 4718596
  190.0 4.1 copy-start.20
  194.1 3.0 copy-start.12
  194.1 3.2 copy-start.2
  198.1 6.1 %copy-start.19 = (bf16[1024,2048]{1,0:T(8,128)(2,1)S(1)}, bf16[1024,2048]{1,0:T(8,128)(2,1)}, u32[]{:S(2)}) copy-start(bf16[1024,2048]{1,0:T(8,128)(2,1)} %get-tuple-element.50) | copy-start | bytes 12582916
  204.2 3.6 copy-start.7
  207.8 2.6 copy-start.11
  214.8 37.3 %copy-start.1 = (bf16[256,512]{1,0:T(8,128)(2,1)S(1)}, bf16[256,512]{1,0:T(8,128)(2,1)}, u32[]{:S(2)}) copy-start(bf16[256,512]{1,0:T(8,128)(2,1)} %refs_1_.2) | copy-start | bytes 786436
  214.8 37.3 %copy-start.3 = (f32[256,512]{1,0:T(8,128)S(1)}, f32[256,512]{1,0:T(8,128)}, u32[]{:S(2)}) copy-start(f32[256,512]{1,0:T(8,128)} %get-tuple-element.47) | copy-start | bytes 1572868
  214.8 37.3 %copy-start.15 = (f32[512]{0:T(512)S(1)}, f32[512]{0:T(512)}, u32[]{:S(2)}) copy-start(f32[512]{0:T(512)} %param.24) | copy-start | bytes 6148
  254.6 187.1 %copy-start = (bf16[256,512]{1,0:T(8,128)(2,1)S(1)}, bf16[256,512]{1,0:T(8,128)(2,1)}, u32[]{:S(2)}) copy-start(bf16[256,512]{1,0:T(8,128)(2,1)} %refs_25_.1) | copy-start | bytes 786436
  254.6 187.1 %copy-start.17 = (f32[512]{0:T(512)S(1)}, f32[512]{0:T(512)}, u32[]{:S(2)}) copy-start(f32[512]{0:T(512)} %param.23) | copy-start | bytes 6148
  441.8 2.7 copy-start.16
  441.8 3.8 copy-start.13
  441.8 3.8 copy-start.14
  444.5 2.3 copy-start.9
  444.5 2.3 copy-start.10
  448.2 1.8 copy-start.8
  450.0 2.2 copy-start.4
  450.0 2.8 copy-start.5

commit v2 on v1

--- a/solution.py
+++ b/solution.py
@@ -101,41 +101,6 @@
     def __init__(self, args, outs, scratch, kinds, steps):
         self.args, self.outs, self.scratch = args, outs, scratch
         self.kinds, self.steps = kinds, steps
-
-
-def run_parts(n_dp, call, *parts):
-    counts = [(len(p.args), len(p.outs), len(p.scratch)) for p in parts]
-    n_in, n_out = sum(c[0] for c in counts), sum(c[1] for c in counts)
-    kinds = set().union(*[p.kinds for p in parts])
-
-    def kernel(*refs):
-        here = Here(n_dp)
-        ins, outs, scratch = refs[:n_in], refs[n_in : n_in + n_out], refs[n_in + n_out :]
-        meet(here, kinds)
-        live = []
-        for part, (a, o, s) in zip(parts, counts):
-            live.append(part.steps(here, ins[:a], outs[:o], scratch[:s]))
-            ins, outs, scratch = ins[a:], outs[o:], scratch[s:]
-        while live:
-            live = [g for g in live if next(g, "end") != "end"]
-
-    vmem = pl.BlockSpec(memory_space=VMEM)
-    results = pl.pallas_call(
-        kernel,
-        out_shape=[o for p in parts for o in p.outs],
-        in_specs=[vmem] * n_in,
-        out_specs=[vmem] * n_out,
-        scratch_shapes=[s for p in parts for s in p.scratch],
-        compiler_params=pltpu.CompilerParams(
-            collective_id=call, has_side_effects=True, vmem_limit_bytes=60 << 20
-        ),
-        name=f"stage_{call}",
-    )(*[x for p in parts for x in p.args])
-    split = []
-    for _, o, _ in counts:
-        split.append(results[:o])
-        results = results[o:]
-    return split
 
 
 def chunked(n, fn):
@@ -427,9 +392,8 @@
             return remote(t_buf.at[i], y_buf.at[i], y_send.at[i], y_recv.at[i], here.over_y)
 
         if use_c:
-            for j in range(2):
-                for i in range(blocks):
-                    core_copy(j, i).start()
+            for i in range(blocks):
+                core_copy(0, i).start()
             yield
             for i in range(blocks):
                 core_copy(0, i).wait_recv()
@@ -443,6 +407,9 @@
 
                 chunked(n, add_core)
                 y_copy(i).start()
+            yield
+            for i in range(blocks):
+                core_copy(1, i).start()
             yield
 
         def up_copy(i, zz):
@@ -585,15 +552,13 @@
 
             chunked(shapes[m][0], keep)
         yield
-        yield
-        yield
         for m in range(count):
             for d in (1, 3, 2):
                 zz = (here.z - d + ROWS) % ROWS
                 copy(m, here.z, zz).wait_recv()
                 if shared:
                     pass_on(m, zz).start()
-            yield
+        yield
         for m in range(count):
             for _, zz, _ in here.others():
                 copy(m, zz, here.z).wait_send()
@@ -635,8 +600,7 @@
                 copy().start()
                 work.append((m, b, h, n, copy))
                 k += 1
-        for _ in range(6):
-            yield
+        yield
         for m, b, h, n, copy in work:
             copy().wait_recv()
 
@@ -648,6 +612,7 @@
                 ).astype(BF16)
 
             chunked(h, add)
+        yield
         for m, b, h, n, copy in work:
             copy().wait_send()
 
@@ -711,15 +676,14 @@
             chunked(shapes[m][0], keep)
             if shared:
                 pass_on(m, here.z).start()
-        for _ in range(4):
-            yield
+        yield
         for m in range(count):
             for d in (1, 3, 2):
                 zz = (here.z - d + ROWS) % ROWS
                 copy(m, here.z, zz).wait_recv()
                 if shared:
                     pass_on(m, zz).start()
-            yield
+        yield
         for m in range(count):
             for _, zz, _ in here.others():
                 copy(m, zz, here.z).wait_send()
@@ -744,8 +708,7 @@
         ]
         for copy in copies:
             copy.start()
-        for _ in range(20):
-            yield
+        yield
         for copy in copies:
             copy.wait()
 
@@ -870,7 +833,7 @@
     return SimpleNamespace(**dict(zip(out_list, results)))
 
 
-def rows_times(o_ref, a_ref, terms, block=256):
+def rows_times(o_ref, a_ref, terms, block=256, first=0, last=None):
     def body(i, _):
         s = pl.ds(pl.multiple_of(i * block, block), block)
         total = None
@@ -880,7 +843,7 @@
         o_ref[s, :] = total.astype(o_ref.dtype)
         return 0
 
-    lax.fori_loop(0, a_ref.shape[0] // block, body, 0)
+    lax.fori_loop(first, last or a_ref.shape[0] // block, body, 0)
 
 
 def columns_times(o_ref, a_ref, b_ref, height=256, width=512):
@@ -1018,6 +981,7 @@
         low = plan.start(pull_low, [i.w_down], [o.w_low])
         make_tables(i.segment, i.inverse, i.sign, o)
         finish(first)
+        cot = plan.start(cot_gather, [i.cotangent], [o.cot_rows])
 
         def normed(b, _):
             s = pl.ds(pl.multiple_of(b * length, length), length)
@@ -1035,9 +999,15 @@
         lax.fori_loop(0, COLS, normed, 0)
         total = plan.start(joint_sum, [plan[p_joint]], [o.joint])
         stat = plan.start(in_stat, [plan[stats]], [plan[got_stats]])
+        advance(low)
+        advance(cot)
+        advance(total)
+        advance(cot, 2)
+        advance(total)
+        advance(cot, 2)
         finish(total)
+        advance(cot)
         finish(stat)
-        cot = plan.start(cot_gather, [i.cotangent], [o.cot_rows])
         summed = plan[got_stats][0] + plan[got_stats][1] + plan[got_stats][2] + plan[got_stats][3]
         o.scale_in[...] = lax.rsqrt(token_major(summed[0:1]) / MODEL_WIDTH + EPSILON)
 
@@ -1049,18 +1019,15 @@
         for _ in attention_forward(i, o):
             pass
         mix = plan.start(mix_gather, [o.mixed], [o.mix_rows])
-        advance(cot, 2)
-        advance(mix)
-        advance(cot, 2)
-        advance(mix)
-        advance(cot, 2)
+        advance(mix, 2)
+        gate = plan.start(pull_gate, [i.w_gate], [o.w_gate_all])
         finish(mix)
-        gate = plan.start(pull_gate, [i.w_gate], [o.w_gate_all])
+        finish(cot)
+        finish(low)
         rows_times(plan[p_out], o.mix_rows, [(ALL, i.w_output, False)])
         out = plan.start(out_sum, [plan[p_out]], [plan[attn_out]])
-        finish(cot)
+        advance(out, 2)
         finish(out)
-        finish_low = low
 
         def add(r, step):
             s = pl.ds(r, step)
@@ -1075,12 +1042,16 @@
         mid = plan.start(
             mid_gather, [plan[gained], plan[own_stat]], [o.mid_rows, plan[mid_stats]]
         )
+        advance(mid, 2)
+        advance(gate)
+        advance(mid)
         up = plan.start(pull_up, [i.w_up], [o.w_up_all])
-        finish(finish_low)
-        advance(mid, 2)
-        rows_times(o.grad_active, o.cot_rows, [(ALL, o.w_low, True)])
-        advance(mid, 2)
-        advance(gate, 4)
+        for k in range(4):
+            rows_times(
+                o.grad_active, o.cot_rows, [(ALL, o.w_low, True)], first=k, last=k + 1
+            )
+            advance(mid)
+        advance(up)
         finish(mid)
         for b in range(COLS):
             summed = plan[mid_stats][b]
@@ -1093,6 +1064,96 @@
         finish(up)
 
     return planned(n_dp, call, "forward", plan, a, outs, body)
+
+
+def middle(n_dp, call, a):
+    two = n_dp == 2
+    length, feats = a.hidden.shape
+    tokens, units = a.grad_active.shape
+    plan = Plan()
+    mid_sum = plan.add(scatter_sum(like((tokens, MODEL_WIDTH), BF16), True, True))
+    inner_stat = plan.add(send_stats(like((COLS, 8, length), F32), plane_stats))
+    d_low = like((units, MODEL_WIDTH), BF16)
+    if two:
+        low_half = plan.add(swap_halves_sum([d_low], [0]))
+        low = plan.buffer(d_low.shape, BF16)
+        d_low = like((units // 2, MODEL_WIDTH), BF16)
+    p_mid = plan.buffer((tokens, MODEL_WIDTH), BF16)
+    d_gate = plan.buffer((tokens, units), BF16)
+    d_up = plan.buffer((tokens, units), BF16)
+    inner = plan.buffer((COLS, 8, length), F32)
+    inners = plan.buffer((ROWS * COLS, 8, length), F32)
+    grad_mid = plan.buffer((length, feats), F32)
+    outs = SimpleNamespace(
+        grad_hidden=like((length, feats), F32),
+        grad_attn=like((length, feats), BF16),
+        gain_mid=like((16, HEAD_SIZE), F32),
+        active=like((tokens, units), BF16),
+        grad_low=d_low,
+        grad_gate=like((MODEL_WIDTH, units), BF16),
+        grad_up=like((MODEL_WIDTH, units), BF16),
+    )
+
+    def body(i, o):
+        here = plan.here
+
+        def tokens_of(b):
+            s = pl.ds(pl.multiple_of(b * length, length), length)
+            scale = i.scale_mid[s, 0:1]
+            gate = dot(i.mid_rows[s, :], i.w_gate_all[...]) * scale
+            upward = dot(i.mid_rows[s, :], i.w_up_all[...]) * scale
+            silu, slope = silu_parts(gate)
+            o.active[s, :] = (silu * upward).astype(BF16)
+            grad = i.grad_active[s, :] * scale
+            grad_gate = (grad * upward * slope).astype(BF16)
+            grad_up = (grad * silu).astype(BF16)
+            plan[d_gate][s, :] = grad_gate
+            plan[d_up][s, :] = grad_up
+            term = grad_gate.astype(F32) * gate + grad_up.astype(F32) * upward
+            plan[inner][b] = lane_major(jnp.sum(term, axis=-1, keepdims=True) * scale)
+            for k in range(ROWS):
+                part = pl.ds(k * feats, feats)
+                plan[p_mid][s, part] = (
+                    dot(grad_gate, i.w_gate_all[part, :], True)
+                    + dot(grad_up, i.w_up_all[part, :], True)
+                ).astype(BF16)
+
+        tokens_of((here.c_core + 2) % COLS)
+        total = plan.start(mid_sum, [plan[p_mid]], [plan[grad_mid]])
+        tokens_of(here.c_y)
+        advance(total)
+        tokens_of(here.c_core)
+        advance(total)
+        tokens_of(here.c)
+        stat = plan.start(inner_stat, [plan[inner]], [plan[inners]])
+        advance(total)
+        low_ref = plan[low] if two else o.grad_low
+        columns_times(low_ref, o.active, i.cot_rows, units)
+        if two:
+            low_sum = plan.start(low_half, [low_ref], [o.grad_low])
+        advance(total)
+        columns_times(o.grad_gate, i.mid_rows, plan[d_gate], width=units)
+        advance(total)
+        columns_times(o.grad_up, i.mid_rows, plan[d_up], width=units)
+        finish(total)
+        finish(stat)
+        summed = plan[inners][0]
+        for k in range(1, ROWS * COLS):
+            summed = summed + plan[inners][k]
+        coef = token_major(summed[0:1] / MODEL_WIDTH)[:, 0:1]
+        grad = plan[grad_mid][...]
+        hidden = i.hidden[...]
+        total = jnp.sum(grad * hidden, axis=0, keepdims=True)
+        o.gain_mid[...] = jnp.zeros((16, HEAD_SIZE), F32)
+        for k in range(feats // HEAD_SIZE):
+            o.gain_mid[4 + k : 5 + k, :] = total[:, k * HEAD_SIZE : (k + 1) * HEAD_SIZE]
+        grad = i.cotangent[...].astype(F32) + grad * i.mlp_gain[...] - hidden * coef
+        o.grad_hidden[...] = grad
+        o.grad_attn[...] = grad.astype(BF16)
+        if two:
+            finish(low_sum)
+
+    return planned(n_dp, call, "middle", plan, a, outs, body)
 
 
 def attention_back(i, grad_mixed, gj_ref, inner_ref, gains_ref, dk_ref, dv_ref):
@@ -1209,22 +1270,23 @@
         attn = plan.start(attn_gather, [i.grad_attn], [plan[attn_rows]])
         low = plan.start(low_push, [i.grad_low], [o.grad_low])
         if two:
-            halves = [
-                plan.start(gate_half, [i.grad_gate], [plan[gate_sum]]),
-                plan.start(up_half, [i.grad_up], [plan[up_sum]]),
-            ]
-        rows_times(plan[p_block], i.active, [(ALL, i.w_low, False)])
+            gate_sums = plan.start(gate_half, [i.grad_gate], [plan[gate_sum]])
+        rows_times(plan[p_block], i.active, [(ALL, i.w_low, False)], first=0, last=3)
         finish(attn)
+        if two:
+            up_sums = plan.start(up_half, [i.grad_up], [plan[up_sum]])
         rows_times(plan[p_mixed], plan[attn_rows], [(ALL, i.w_output, True)])
         mixed = plan.start(mixed_sum, [plan[p_mixed]], [plan[grad_mixed]])
+        rows_times(plan[p_block], i.active, [(ALL, i.w_low, False)], first=3, last=4)
         block = plan.start(block_sum, [plan[p_block]], [o.block])
-        columns_times(o.d_output, i.mix_rows, plan[attn_rows])
+        advance(mixed)
+        advance(low)
+        advance(block, 2)
         if two:
-            swap_output = plan.start(output_swap, [o.d_output], [o.d_output_other])
+            advance(gate_sums)
+        advance(mixed)
+        gate = plan.start(gate_push, [plan[gate_sum] if two else i.grad_gate], [o.grad_gate])
         finish(mixed)
-        if two:
-            finish(halves[0])
-        gate = plan.start(gate_push, [plan[gate_sum] if two else i.grad_gate], [o.grad_gate])
         plan[gain_rows][...] = i.gain_mid[...]
         attention_back(
             i,
@@ -1237,12 +1299,19 @@
         )
         joint = plan.start(joint_gather, [plan[joint_in]], [plan[joint_rows]])
         stat = plan.start(in_stat, [plan[inner]], [o.in_inners])
-        finish(low)
+        columns_times(o.d_output, i.mix_rows, plan[attn_rows])
+        if two:
+            swap_output = plan.start(output_swap, [o.d_output], [o.d_output_other])
         advance(block)
+        advance(joint)
         if two:
-            finish(halves[1])
+            advance(up_sums)
+        advance(block)
+        advance(gate)
+        advance(joint)
+        up = plan.start(up_push, [plan[up_sum] if two else i.grad_up], [o.grad_up])
+        advance(block)
         finish(joint)
-        up = plan.start(up_push, [plan[up_sum] if two else i.grad_up], [o.grad_up])
         columns_times(o.d_joint, i.in_gained, plan[joint_rows])
         if two:
             swap_joint = plan.start(joint_swap, [o.d_joint], [o.d_joint_other])
@@ -1256,7 +1325,9 @@
             ],
         )
         grad_in = plan.start(in_sum, [plan[p_in]], [o.grad_in])
-        finish(gate)
+        advance(grad_in)
+        advance(block)
+        advance(up)
         finish(grad_in)
         total = jnp.sum(o.grad_in[...] * i.layer_input[...].astype(F32), axis=0, keepdims=True)
         for k in range(feats // HEAD_SIZE):
@@ -1265,8 +1336,12 @@
         finish(block)
         finish(gains)
         finish(stat)
+        finish(low)
+        finish(gate)
         finish(up)
         if two:
+            finish(gate_sums)
+            finish(up_sums)
             finish(swap_output)
             finish(swap_joint)
 
@@ -1334,43 +1409,29 @@
             sign=jnp.concatenate([-ones, ones])[None],
         ),
     )
-    scale_mid = f.scale_mid[:, 0:1]
-    gate = dot(f.mid_rows, f.w_gate_all) * scale_mid
-    upward = dot(f.mid_rows, f.w_up_all) * scale_mid
-    silu, slope = silu_parts(gate)
-    active = (silu * upward).astype(BF16)
-    grad_gated = f.grad_active * scale_mid
-    grad_gate_in = (grad_gated * upward * slope).astype(BF16)
-    grad_up_in = (grad_gated * silu).astype(BF16)
-    mid_inner = jnp.sum(
-        grad_gate_in.astype(F32) * gate + grad_up_in.astype(F32) * upward, axis=-1, keepdims=True
+    m = middle(
+        dp,
+        1,
+        SimpleNamespace(
+            mid_rows=f.mid_rows,
+            cot_rows=f.cot_rows,
+            grad_active=f.grad_active,
+            scale_mid=f.scale_mid,
+            w_gate_all=f.w_gate_all,
+            w_up_all=f.w_up_all,
+            hidden=f.hidden,
+            cotangent=cotangent,
+            mlp_gain=mlp_gain[None],
+        ),
     )
-    grad_low = weight_term(active, f.cot_rows).astype(BF16)
-    grad_mid_part = dot(grad_gate_in, f.w_gate_all, True) + dot(grad_up_in, f.w_up_all, True)
-    parts = [
-        scatter_sum(grad_mid_part.astype(BF16), True, True),
-        send_stats((mid_inner * scale_mid).reshape(COLS, 2, HEAD_SIZE), plane_stats),
-    ]
-    if two:
-        parts.append(swap_halves_sum([grad_low], [0]))
-    else:
-        grad_low = lax.psum(grad_low, "dp")
-    (grad_mid,), (mid_inners,), *low = run_parts(dp, 1, *parts)
-    if two:
-        ((grad_low,),) = low
-    grad_gate = weight_term(f.mid_rows, grad_gate_in).astype(BF16)
-    grad_up = weight_term(f.mid_rows, grad_up_in).astype(BF16)
-    mid_coef = jnp.sum(mid_inners, axis=0).reshape(length, 1) / MODEL_WIDTH
-    gain_mid = jnp.sum(grad_mid * f.hidden, axis=0)
-    grad_hidden = cotangent.astype(F32) + grad_mid * mlp_gain - f.hidden * mid_coef
-    grad_attn = grad_hidden.astype(BF16)
+    grad_low, grad_gate, grad_up = m.grad_low, m.grad_gate, m.grad_up
     if not two:
-        grad_gate, grad_up = lax.psum(grad_gate, "dp"), lax.psum(grad_up, "dp")
+        grad_low, grad_gate, grad_up = lax.psum((grad_low, grad_gate, grad_up), "dp")
     b = backward(
         dp,
         2,
         SimpleNamespace(
-            grad_attn=grad_attn,
+            grad_attn=m.grad_attn,
             w_output=w_output,
             w_query=w_query,
             key_matrix=key_matrix,
@@ -1389,12 +1450,12 @@
             key_gain=key_gain[None],
             mix_rows=f.mix_rows,
             in_gained=f.in_gained,
-            active=active,
+            active=m.active,
             w_low=f.w_low,
             grad_gate=grad_gate,
             grad_up=grad_up,
             grad_low=grad_low,
-            gain_mid=jnp.pad(gain_mid.reshape(-1, HEAD_SIZE), ((4, 8), (0, 0))),
+            gain_mid=m.gain_mid,
             layer_input=layer_input,
         ),
     )
@@ -1405,7 +1466,7 @@
         grad_output, grad_joint = lax.psum((b.d_output, b.d_joint), "dp")
         grad_output, grad_joint = grad_output.astype(F32), grad_joint.astype(F32)
     in_coef = jnp.sum(b.in_inners[:, 0], axis=0).reshape(length, 1) / MODEL_WIDTH
-    input_grad = grad_hidden + b.grad_in * attn_gain - layer_input.astype(F32) * in_coef
+    input_grad = m.grad_hidden + b.grad_in * attn_gain - layer_input.astype(F32) * in_coef
     return (
         (f.hidden + b.block).astype(BF16),
         input_grad,

time: 457 us -> 390 us (0.85)
  Pallas kernels: 405 us -> 373 us
  matrix products: 28.8 us -> 0 us
    pallas_call x1 -> x0, Pallas kernels: 36.6 us -> none  [run_parts(): pl.pallas_call(kernel, out_shape=[o for p in parts for o in p.outs], in_s...]
    dot_general x7 -> x0, matrix products: 28.8 us -> none  [the longest x4 16.1 us: dot(): lax.dot_general(left, right, (((1,), (1 if flipped else 0,)), ((), ())),...]
    pallas_call x2 -> x3, Pallas kernels: 369 us -> 373 us  [planned(): pl.pallas_call(kernel, out_shape=list(out_list.values()), in_specs=[vmem]...]
where the time goes in v2:
time: 390 us
  Pallas kernels  373 us (96%)
  other arithmetic  11.9 us (3%)
  local copies, waits for them, and re-layouts  4.11 us (1%)
    pallas_call x3, Pallas kernels, planned(): pl.pallas_call(kernel, out_shape=list(out_list.values()), in_specs=[vmem]...  373 us

profile of v2, /device:TPU:0, one launch (start us, length us, event | category | flops | bytes accessed | tf_op | source)
XLA Modules:
  0.0 390.0 jit_solution(10071262627185040698)
XLA Ops:
  0.7 0.6 maximum_bitcast_fusion.refs_14_
  1.2 167.8 %forward.1 = (bf16[1024,512]{1,0:T(8,128)(2,1)}, f32[256,1024]{1,0:T(8,128)}, f32[256,128]{1,0:T(8,128)}, f32[256,256]{1,0:T(8,128)}, f32[256,128]{1,0:T(8,128)}...) custom-call(bf16[256,512]{1,0:T(8,128)(2,1)} %refs_25_.1, ...), custom_call_target="tpu_custom_call" | custom-call | tf_op jit(solution)/shard_map/forward/pallas_call | solution.py:822
  169.1 43.1 %middle.1 = (f32[256,512]{1,0:T(8,128)}, bf16[256,512]{1,0:T(8,128)(2,1)}, f32[16,128]{1,0:T(8,128)}, bf16[1024,384]{1,0:T(8,128)(2,1)}, bf16[192,2048]{1,0:T(8,...) custom-call(bf16[1024,2048]{1,0:T(8,128)(2,1)} %get-tuple-element.52.refs_0_, ...), custom_call_target="tpu_custom_call" | custom-call | tf_op jit(solution)/shard_map/middle/pallas_call | solution.py:822
  212.2 0.0 copy-start
  212.2 0.0 copy-start.1
  212.3 0.0 copy-start.10
  212.3 162.3 %backward.1 = (f32[256,512]{1,0:T(8,128)}, f32[4,8,256]{2,1,0:T(8,128)}, f32[256,512]{1,0:T(8,128)}, bf16[2,256,1536]{2,1,0:T(8,128)(2,1)}, bf16[2,256,1536]{2,1...) custom-call(bf16[256,512]{1,0:T(8,128)(2,1)} %get-tuple-element.58.r, ...), custom_call_target="tpu_custom_call" | custom-call | tf_op jit(solution)/shard_map/backward/pallas_call | solution.py:822
  374.5 0.8 slice_reduce_fusion
  375.3 0.0 copy-done
  375.3 0.0 copy-done.1
  375.3 0.0 copy-done.10
  375.4 2.5 multiply_subtract_fusion
  377.9 0.5 slice_reduce_fusion.1
  378.4 0.6 fusion.1
  379.0 0.0 copy-done.7
  379.0 1.1 convert_add_fusion.1
  380.1 0.4 convert_add_fusion
  380.5 1.1 slice.32
  381.6 1.0 fusion
  382.6 0.7 copy-done.4
  383.4 2.2 bitcast_convert_fusion
  385.6 0.0 copy-done.2
  385.6 0.6 copy-done.3
  386.2 3.8 bitcast_convert_fusion.1
  (14 shorter events, 0.0 us)
Async XLA Ops:
  212.2 163.1 %copy-start = (bf16[256,512]{1,0:T(8,128)(2,1)S(1)}, bf16[256,512]{1,0:T(8,128)(2,1)}, u32[]{:S(2)}) copy-start(bf16[256,512]{1,0:T(8,128)(2,1)} %refs_25_.1) | copy-start | bytes 786436
  212.2 163.1 %copy-start.1 = (f32[256,512]{1,0:T(8,128)S(1)}, f32[256,512]{1,0:T(8,128)}, u32[]{:S(2)}) copy-start(f32[256,512]{1,0:T(8,128)} %get-tuple-element.51.refs_6_) | copy-start | bytes 1572868
  212.3 163.1 %copy-start.10 = (f32[512]{0:T(512)S(1)}, f32[512]{0:T(512)}, u32[]{:S(2)}) copy-start(f32[512]{0:T(512)} %param.23) | copy-start | bytes 6148
  375.4 2.5 copy-start.9
  375.4 3.6 copy-start.7
  375.4 3.6 copy-start.8
  377.9 2.3 copy-start.5
  377.9 2.3 copy-start.6
  381.6 1.8 copy-start.4
  383.4 2.2 copy-start.2
  383.4 2.8 copy-start.3

commit v3 on v2

--- a/solution.py
+++ b/solution.py
@@ -542,9 +542,6 @@
             return remote(region, region, dp_send.at[k], dp_recv.at[k], here.over_dp)
 
         for m in range(count):
-            for _, zz, _ in here.others():
-                copy(m, zz, here.z).start()
-        for m in range(count):
             from_place, to_place = source(m, here.z, False), target(m, here.z, False)
 
             def keep(r, step, m=m, from_place=from_place, to_place=to_place):
@@ -552,13 +549,16 @@
 
             chunked(shapes[m][0], keep)
         yield
-        for m in range(count):
-            for d in (1, 3, 2):
-                zz = (here.z - d + ROWS) % ROWS
+        for d in (2, 1, 3):
+            for m in range(count):
+                copy(m, (here.z + d) % ROWS, here.z).start()
+            yield
+        for _, _, zz in here.others():
+            for m in range(count):
                 copy(m, here.z, zz).wait_recv()
                 if shared:
                     pass_on(m, zz).start()
-        yield
+            yield
         for m in range(count):
             for _, zz, _ in here.others():
                 copy(m, zz, here.z).wait_send()
@@ -833,17 +833,17 @@
     return SimpleNamespace(**dict(zip(out_list, results)))
 
 
-def rows_times(o_ref, a_ref, terms, block=256, first=0, last=None):
+def rows_times(o_ref, terms, block=256, first=0, last=None):
     def body(i, _):
         s = pl.ds(pl.multiple_of(i * block, block), block)
         total = None
-        for columns, b_ref, flipped in terms:
+        for a_ref, columns, b_ref, flipped in terms:
             term = dot(a_ref[s, columns], b_ref[...], flipped)
             total = term if total is None else total + term
         o_ref[s, :] = total.astype(o_ref.dtype)
         return 0
 
-    lax.fori_loop(first, last or a_ref.shape[0] // block, body, 0)
+    lax.fori_loop(first, last or o_ref.shape[0] // block, body, 0)
 
 
 def columns_times(o_ref, a_ref, b_ref, height=256, width=512):
@@ -979,6 +979,7 @@
     def body(i, o):
         first = plan.start(in_gather, [i.layer_input], [plan[in_rows]])
         low = plan.start(pull_low, [i.w_down], [o.w_low])
+        advance(low, 3)
         make_tables(i.segment, i.inverse, i.sign, o)
         finish(first)
         cot = plan.start(cot_gather, [i.cotangent], [o.cot_rows])
@@ -999,7 +1000,7 @@
         lax.fori_loop(0, COLS, normed, 0)
         total = plan.start(joint_sum, [plan[p_joint]], [o.joint])
         stat = plan.start(in_stat, [plan[stats]], [plan[got_stats]])
-        advance(low)
+        advance(low, 3)
         advance(cot)
         advance(total)
         advance(cot, 2)
@@ -1021,10 +1022,11 @@
         mix = plan.start(mix_gather, [o.mixed], [o.mix_rows])
         advance(mix, 2)
         gate = plan.start(pull_gate, [i.w_gate], [o.w_gate_all])
+        advance(gate, 3)
         finish(mix)
         finish(cot)
         finish(low)
-        rows_times(plan[p_out], o.mix_rows, [(ALL, i.w_output, False)])
+        rows_times(plan[p_out], [(o.mix_rows, ALL, i.w_output, False)])
         out = plan.start(out_sum, [plan[p_out]], [plan[attn_out]])
         advance(out, 2)
         finish(out)
@@ -1043,15 +1045,14 @@
             mid_gather, [plan[gained], plan[own_stat]], [o.mid_rows, plan[mid_stats]]
         )
         advance(mid, 2)
-        advance(gate)
+        advance(gate, 3)
         advance(mid)
         up = plan.start(pull_up, [i.w_up], [o.w_up_all])
+        advance(up, 3)
         for k in range(4):
-            rows_times(
-                o.grad_active, o.cot_rows, [(ALL, o.w_low, True)], first=k, last=k + 1
-            )
+            rows_times(o.grad_active, [(o.cot_rows, ALL, o.w_low, True)], first=k, last=k + 1)
             advance(mid)
-        advance(up)
+        advance(up, 3)
         finish(mid)
         for b in range(COLS):
             summed = plan[mid_stats][b]
@@ -1156,13 +1157,19 @@
     return planned(n_dp, call, "middle", plan, a, outs, body)
 
 
-def attention_back(i, grad_mixed, gj_ref, inner_ref, gains_ref, dk_ref, dv_ref):
+def attention_back(i, grad_mixed, gq_ref, gkv_ref, inner_ref, gains_ref, dk_ref, dv_ref):
     heads, groups = i.q.shape[1] // HEAD_SIZE, i.k.shape[1] // HEAD_SIZE
     each = heads // groups
     scale = HEAD_SIZE ** (-0.5)
     cosine, sine = i.cosine[...], i.sine[...]
     scale_in = i.scale_in[:, 0:1]
     inner = jnp.zeros((i.q.shape[0], HEAD_SIZE), F32)
+
+    def put(at_head, out):
+        if at_head < heads:
+            gq_ref[:, pl.ds(at_head * HEAD_SIZE, HEAD_SIZE)] = out
+        else:
+            gkv_ref[:, pl.ds((at_head - heads) * HEAD_SIZE, HEAD_SIZE)] = out
 
     def norm_back(grad_rot, at_head, gain):
         grad = grad_rot * cosine - swapped(grad_rot) * sine
@@ -1172,7 +1179,7 @@
         u = grad * gain
         back = norm * (u - unit * jnp.mean(u * unit, axis=-1, keepdims=True))
         out = (back * scale_in).astype(BF16)
-        gj_ref[:, pl.ds(at_head * HEAD_SIZE, HEAD_SIZE)] = out
+        put(at_head, out)
         return out.astype(F32) * raw, jnp.sum(grad * unit, axis=0, keepdims=True)
 
     gain_q = jnp.zeros((1, HEAD_SIZE), F32)
@@ -1204,7 +1211,7 @@
         gain_k = gain_k + gain
         at_head = heads + groups + g
         out = (dv_ref[...] * scale_in).astype(BF16)
-        gj_ref[:, pl.ds(at_head * HEAD_SIZE, HEAD_SIZE)] = out
+        put(at_head, out)
         inner = inner + out.astype(F32) * head_at(i.joint, at_head)
     gains_ref[8:9, :] = gain_q
     gains_ref[9:10, :] = gain_k
@@ -1215,12 +1222,12 @@
     two = n_dp == 2
     length, feats = a.grad_attn.shape
     query_width, key_width = a.w_query.shape[1], a.key_matrix.shape[1]
-    wide = query_width + 2 * key_width
     tokens = length * COLS
     plan = Plan()
     attn_gather = plan.add(gather(a.grad_attn, False, True))
     mixed_sum = plan.add(scatter_sum(like((tokens, feats), BF16), True, False, BF16))
-    joint_gather = plan.add(gather(like((length, wide), BF16), True, False))
+    q_gather = plan.add(gather(like((length, query_width), BF16), True, False))
+    kv_gather = plan.add(gather(like((length, 2 * key_width), BF16), True, False))
     in_sum = plan.add(scatter_sum(like((tokens, feats), BF16), False, True))
     in_stat = plan.add(send_stats(like((1, 8, length), F32), owner_stats))
     block_sum = plan.add(scatter_sum(like((tokens, MODEL_WIDTH), BF16), True, True))
@@ -1238,15 +1245,19 @@
     ]
     gate_push, up_push, low_push = [plan.add(p) for p in pushes]
     gain_sum = plan.add(sum_gains(like((16, HEAD_SIZE), F32), n_dp))
-    d_output, d_joint = like((feats, feats), BF16), like((feats, wide), BF16)
+    d_output, d_q = like((feats, feats), BF16), like((feats, query_width), BF16)
+    d_kv = like((feats, 2 * key_width), BF16)
     if two:
         output_swap = plan.add(swap([d_output]))
-        joint_swap = plan.add(swap([d_joint]))
+        q_swap = plan.add(swap([d_q]))
+        kv_swap = plan.add(swap([d_kv]))
     attn_rows = plan.buffer((tokens, feats), BF16)
     p_mixed = plan.buffer((tokens, feats), BF16)
     grad_mixed = plan.buffer((length, feats), BF16)
-    joint_in = plan.buffer((length, wide), BF16)
-    joint_rows = plan.buffer((tokens, wide), BF16)
+    q_in = plan.buffer((length, query_width), BF16)
+    kv_in = plan.buffer((length, 2 * key_width), BF16)
+    q_rows = plan.buffer((tokens, query_width), BF16)
+    kv_rows = plan.buffer((tokens, 2 * key_width), BF16)
     p_in = plan.buffer((tokens, feats), BF16)
     p_block = plan.buffer((tokens, MODEL_WIDTH), BF16)
     inner = plan.buffer((1, 8, length), F32)
@@ -1261,27 +1272,28 @@
         grad_low=pushes[2].outs[0],
         gains=like((ROWS, 16, HEAD_SIZE), F32),
         d_output=d_output,
-        d_joint=d_joint,
+        d_q=d_q,
+        d_kv=d_kv,
     )
     if two:
-        outs.d_output_other, outs.d_joint_other = d_output, d_joint
+        outs.d_output_other, outs.d_q_other, outs.d_kv_other = d_output, d_q, d_kv
 
     def body(i, o):
         attn = plan.start(attn_gather, [i.grad_attn], [plan[attn_rows]])
         low = plan.start(low_push, [i.grad_low], [o.grad_low])
         if two:
             gate_sums = plan.start(gate_half, [i.grad_gate], [plan[gate_sum]])
-        rows_times(plan[p_block], i.active, [(ALL, i.w_low, False)], first=0, last=3)
+        rows_times(plan[p_block], [(i.active, ALL, i.w_low, False)], first=0, last=3)
         finish(attn)
         if two:
             up_sums = plan.start(up_half, [i.grad_up], [plan[up_sum]])
-        rows_times(plan[p_mixed], plan[attn_rows], [(ALL, i.w_output, True)])
+        rows_times(plan[p_mixed], [(plan[attn_rows], ALL, i.w_output, True)])
         mixed = plan.start(mixed_sum, [plan[p_mixed]], [plan[grad_mixed]])
-        rows_times(plan[p_block], i.active, [(ALL, i.w_low, False)], first=3, last=4)
+        rows_times(plan[p_block], [(i.active, ALL, i.w_low, False)], first=3, last=4)
         block = plan.start(block_sum, [plan[p_block]], [o.block])
         advance(mixed)
+        advance(block, 2)
         advance(low)
-        advance(block, 2)
         if two:
             advance(gate_sums)
         advance(mixed)
@@ -1291,37 +1303,41 @@
         attention_back(
             i,
             plan[grad_mixed],
-            plan[joint_in],
+            plan[q_in],
+            plan[kv_in],
             plan[inner],
             plan[gain_rows],
             plan[dk],
             plan[dv],
         )
-        joint = plan.start(joint_gather, [plan[joint_in]], [plan[joint_rows]])
+        kv = plan.start(kv_gather, [plan[kv_in]], [plan[kv_rows]])
+        q = plan.start(q_gather, [plan[q_in]], [plan[q_rows]])
         stat = plan.start(in_stat, [plan[inner]], [o.in_inners])
+        if two:
+            advance(up_sums)
+        advance(kv)
+        advance(gate)
         columns_times(o.d_output, i.mix_rows, plan[attn_rows])
         if two:
             swap_output = plan.start(output_swap, [o.d_output], [o.d_output_other])
-        advance(block)
-        advance(joint)
+        advance(q)
+        advance(kv)
+        advance(q)
+        finish(kv)
+        up = plan.start(up_push, [plan[up_sum] if two else i.grad_up], [o.grad_up])
+        columns_times(o.d_kv, i.in_gained, plan[kv_rows])
         if two:
-            advance(up_sums)
-        advance(block)
-        advance(gate)
-        advance(joint)
-        up = plan.start(up_push, [plan[up_sum] if two else i.grad_up], [o.grad_up])
-        advance(block)
-        finish(joint)
-        columns_times(o.d_joint, i.in_gained, plan[joint_rows])
+            swap_kv = plan.start(kv_swap, [o.d_kv], [o.d_kv_other])
+        finish(q)
+        columns_times(o.d_q, i.in_gained, plan[q_rows])
         if two:
-            swap_joint = plan.start(joint_swap, [o.d_joint], [o.d_joint_other])
+            swap_q = plan.start(q_swap, [o.d_q], [o.d_q_other])
         rows_times(
             plan[p_in],
-            plan[joint_rows],
             [
-                (pl.ds(0, query_width), i.w_query, True),
-                (pl.ds(query_width, key_width), i.key_matrix, True),
-                (pl.ds(query_width + key_width, key_width), i.value_matrix, True),
+                (plan[q_rows], ALL, i.w_query, True),
+                (plan[kv_rows], pl.ds(0, key_width), i.key_matrix, True),
+                (plan[kv_rows], pl.ds(key_width, key_width), i.value_matrix, True),
             ],
         )
         grad_in = plan.start(in_sum, [plan[p_in]], [o.grad_in])
@@ -1343,7 +1359,8 @@
             finish(gate_sums)
             finish(up_sums)
             finish(swap_output)
-            finish(swap_joint)
+            finish(swap_kv)
+            finish(swap_q)
 
     return planned(n_dp, call, "backward", plan, a, outs, body)
 
@@ -1381,7 +1398,7 @@
     segment_ids,
 ):
     length, feats = layer_input.shape
-    query_width, key_width = w_query.shape[1], key_matrix.shape[1]
+    key_width = key_matrix.shape[1]
     ff_local = w_gate.shape[1]
     two = dp == 2
     half = jnp.arange(HEAD_SIZE // 2, dtype=F32)
@@ -1461,18 +1478,19 @@
     )
     if two:
         grad_output = b.d_output.astype(F32) + b.d_output_other.astype(F32)
-        grad_joint = b.d_joint.astype(F32) + b.d_joint_other.astype(F32)
+        grad_query = b.d_q.astype(F32) + b.d_q_other.astype(F32)
+        grad_kv = b.d_kv.astype(F32) + b.d_kv_other.astype(F32)
     else:
-        grad_output, grad_joint = lax.psum((b.d_output, b.d_joint), "dp")
-        grad_output, grad_joint = grad_output.astype(F32), grad_joint.astype(F32)
+        sums = lax.psum((b.d_output, b.d_q, b.d_kv), "dp")
+        grad_output, grad_query, grad_kv = [term.astype(F32) for term in sums]
     in_coef = jnp.sum(b.in_inners[:, 0], axis=0).reshape(length, 1) / MODEL_WIDTH
     input_grad = m.grad_hidden + b.grad_in * attn_gain - layer_input.astype(F32) * in_coef
     return (
         (f.hidden + b.block).astype(BF16),
         input_grad,
-        grad_joint[:, :query_width],
-        grad_joint[:, query_width : query_width + key_width],
-        grad_joint[:, query_width + key_width :],
+        grad_query,
+        grad_kv[:, :key_width],
+        grad_kv[:, key_width:],
         grad_output,
         b.grad_gate.reshape(feats, ff_local).astype(F32),
         b.grad_up.reshape(feats, ff_local).astype(F32),

time: 390 us -> 372 us (0.954)
  Pallas kernels: 373 us -> 354 us
    pallas_call x3, Pallas kernels: 373 us -> 354 us  [planned(): pl.pallas_call(kernel, out_shape=list(out_list.values()), in_specs=[vmem]...]
where the time goes in v3:
time: 372 us; the launch traced here: 371 us
  Pallas kernels  354 us (95%)
  other arithmetic  12.7 us (3%)
    pallas_call x3, Pallas kernels, planned(): pl.pallas_call(kernel, out_shape=list(out_list.values()), in_specs=[vmem]...  354 us

profile of v3, /device:TPU:0, one launch (start us, length us, event | category | flops | bytes accessed | tf_op | source)
XLA Modules:
  0.0 371.1 jit_solution(8900050182110247945)
XLA Ops:
  0.7 0.6 maximum_bitcast_fusion.refs_14_
  1.2 166.9 %forward.1 = (bf16[1024,512]{1,0:T(8,128)(2,1)}, f32[256,1024]{1,0:T(8,128)}, f32[256,128]{1,0:T(8,128)}, f32[256,256]{1,0:T(8,128)}, f32[256,128]{1,0:T(8,128)}...) custom-call(bf16[256,512]{1,0:T(8,128)(2,1)} %refs_25_.1, ...), custom_call_target="tpu_custom_call" | custom-call | tf_op jit(solution)/shard_map/forward/pallas_call | solution.py:822
  168.2 46.4 %middle.1 = (f32[256,512]{1,0:T(8,128)}, bf16[256,512]{1,0:T(8,128)(2,1)}, f32[16,128]{1,0:T(8,128)}, bf16[1024,384]{1,0:T(8,128)(2,1)}, bf16[192,2048]{1,0:T(8,...) custom-call(bf16[1024,2048]{1,0:T(8,128)(2,1)} %get-tuple-element.54.refs_0_, ...), custom_call_target="tpu_custom_call" | custom-call | tf_op jit(solution)/shard_map/middle/pallas_call | solution.py:822
  214.6 0.0 copy-start
  214.6 0.0 copy-start.1
  214.6 0.0 copy-start.12
  214.7 141.1 %backward.1 = (f32[256,512]{1,0:T(8,128)}, f32[4,8,256]{2,1,0:T(8,128)}, f32[256,512]{1,0:T(8,128)}, bf16[2,256,1536]{2,1,0:T(8,128)(2,1)}, bf16[2,256,1536]{2,1...) custom-call(bf16[256,512]{1,0:T(8,128)(2,1)} %get-tuple-element.60.r, ...), custom_call_target="tpu_custom_call" | custom-call | tf_op jit(solution)/shard_map/backward/pallas_call | solution.py:822
  355.8 0.8 slice_reduce_fusion
  356.6 0.0 copy-done
  356.6 0.0 copy-done.1
  356.6 0.0 copy-done.12
  356.6 0.0 copy-start.11
  356.6 0.0 copy-start.5
  356.6 0.0 copy-start.6
  356.6 2.5 multiply_subtract_fusion
  359.1 0.5 slice_reduce_fusion.1
  359.7 0.6 fusion.1
  360.3 1.1 convert_add_fusion.2
  361.4 1.2 convert_add_fusion
  362.7 1.0 fusion
  363.7 0.8 copy-done.4
  364.5 2.2 bitcast_convert_fusion
  366.7 0.6 copy-done.3
  367.3 3.8 %bitcast_convert_fusion.1 = (f32[512,1536]{1,0:T(8,128)}, f32[512,1536]{1,0:T(8,128)}) fusion(bf16[2,256,1536]{2,1,0:T(8,128)(2,1)S(1)} %copy-done.3, bf16[2,256,1536]{2,1,0:T(8,128)(2,1)S(1)} %copy-done.2), kind=kLoop, calls=%fused_computation.1 | loop fusion | flops 1572864 | bytes 9437184 | tf_op jit(solution)/shard_map/convert_element_type | solution.py:1496
  (17 shorter events, 0.0 us)
Async XLA Ops:
  214.6 142.0 %copy-start = (bf16[256,512]{1,0:T(8,128)(2,1)S(1)}, bf16[256,512]{1,0:T(8,128)(2,1)}, u32[]{:S(2)}) copy-start(bf16[256,512]{1,0:T(8,128)(2,1)} %refs_25_.1) | copy-start | bytes 786436
  214.6 142.0 %copy-start.1 = (f32[256,512]{1,0:T(8,128)S(1)}, f32[256,512]{1,0:T(8,128)}, u32[]{:S(2)}) copy-start(f32[256,512]{1,0:T(8,128)} %get-tuple-element.53.refs_6_) | copy-start | bytes 1572868
  214.6 142.0 %copy-start.12 = (f32[512]{0:T(512)S(1)}, f32[512]{0:T(512)}, u32[]{:S(2)}) copy-start(f32[512]{0:T(512)} %param.23) | copy-start | bytes 6148
  356.6 2.5 copy-start.11
  356.6 3.7 copy-start.5
  356.6 3.7 copy-start.6
  359.1 2.3 copy-start.7
  359.1 2.3 copy-start.8
  359.1 2.3 copy-start.9
  359.1 2.3 copy-start.10
  362.7 1.8 copy-start.4
  364.5 2.2 copy-start.2
  364.5 2.8 copy-start.3

commit v4 on v3

--- a/solution.py
+++ b/solution.py
@@ -1297,7 +1297,6 @@
         if two:
             advance(gate_sums)
         advance(mixed)
-        gate = plan.start(gate_push, [plan[gate_sum] if two else i.grad_gate], [o.grad_gate])
         finish(mixed)
         plan[gain_rows][...] = i.gain_mid[...]
         attention_back(
@@ -1316,7 +1315,7 @@
         if two:
             advance(up_sums)
         advance(kv)
-        advance(gate)
+        gate = plan.start(gate_push, [plan[gate_sum] if two else i.grad_gate], [o.grad_gate])
         columns_times(o.d_output, i.mix_rows, plan[attn_rows])
         if two:
             swap_output = plan.start(output_swap, [o.d_output], [o.d_output_other])
@@ -1324,6 +1323,7 @@
         advance(kv)
         advance(q)
         finish(kv)
+        advance(gate)
         up = plan.start(up_push, [plan[up_sum] if two else i.grad_up], [o.grad_up])
         columns_times(o.d_kv, i.in_gained, plan[kv_rows])
         if two:

time: 372 us -> 380 us (1.022)
  Pallas kernels: 354 us -> 363 us
    pallas_call x3, Pallas kernels: 354 us -> 363 us  [planned(): pl.pallas_call(kernel, out_shape=list(out_list.values()), in_specs=[vmem]...]
where the time goes in v4:
time: 380 us
  Pallas kernels  363 us (96%)
  other arithmetic  12.7 us (3%)
    pallas_call x3, Pallas kernels, planned(): pl.pallas_call(kernel, out_shape=list(out_list.values()), in_specs=[vmem]...  363 us

profile of v4, /device:TPU:0, one launch (start us, length us, event | category | flops | bytes accessed | tf_op | source)
XLA Modules:
  0.0 379.6 jit_solution(7602961090866331991)
XLA Ops:
  0.7 0.6 maximum_bitcast_fusion.refs_14_
  1.2 166.9 %forward.1 = (bf16[1024,512]{1,0:T(8,128)(2,1)}, f32[256,1024]{1,0:T(8,128)}, f32[256,128]{1,0:T(8,128)}, f32[256,256]{1,0:T(8,128)}, f32[256,128]{1,0:T(8,128)}...) custom-call(bf16[256,512]{1,0:T(8,128)(2,1)} %refs_25_.1, ...), custom_call_target="tpu_custom_call" | custom-call | tf_op jit(solution)/shard_map/forward/pallas_call | solution.py:822
  168.2 46.4 %middle.1 = (f32[256,512]{1,0:T(8,128)}, bf16[256,512]{1,0:T(8,128)(2,1)}, f32[16,128]{1,0:T(8,128)}, bf16[1024,384]{1,0:T(8,128)(2,1)}, bf16[192,2048]{1,0:T(8,...) custom-call(bf16[1024,2048]{1,0:T(8,128)(2,1)} %get-tuple-element.54.refs_0_, ...), custom_call_target="tpu_custom_call" | custom-call | tf_op jit(solution)/shard_map/middle/pallas_call | solution.py:822
  214.6 0.0 copy-start
  214.6 0.0 copy-start.1
  214.6 0.0 copy-start.12
  214.7 149.7 %backward.1 = (f32[256,512]{1,0:T(8,128)}, f32[4,8,256]{2,1,0:T(8,128)}, f32[256,512]{1,0:T(8,128)}, bf16[2,256,1536]{2,1,0:T(8,128)(2,1)}, bf16[2,256,1536]{2,1...) custom-call(bf16[256,512]{1,0:T(8,128)(2,1)} %get-tuple-element.60.r, ...), custom_call_target="tpu_custom_call" | custom-call | tf_op jit(solution)/shard_map/backward/pallas_call | solution.py:822
  364.4 0.8 slice_reduce_fusion
  365.2 0.0 copy-done
  365.2 0.0 copy-done.1
  365.2 2.5 multiply_subtract_fusion
  367.7 0.0 copy-done.11
  367.7 0.5 slice_reduce_fusion.1
  368.3 0.6 fusion.1
  368.9 0.0 copy-done.6
  368.9 1.1 convert_add_fusion.2
  370.0 0.0 copy-done.7
  370.0 1.2 convert_add_fusion
  371.3 1.0 fusion
  372.3 0.8 copy-done.4
  373.0 2.2 bitcast_convert_fusion
  375.3 0.0 copy-done.2
  375.3 0.6 copy-done.3
  375.9 3.8 bitcast_convert_fusion.1
  (17 shorter events, 0.0 us)
Async XLA Ops:
  214.6 150.5 %copy-start = (bf16[256,512]{1,0:T(8,128)(2,1)S(1)}, bf16[256,512]{1,0:T(8,128)(2,1)}, u32[]{:S(2)}) copy-start(bf16[256,512]{1,0:T(8,128)(2,1)} %refs_25_.1) | copy-start | bytes 786436
  214.6 150.5 %copy-start.1 = (f32[256,512]{1,0:T(8,128)S(1)}, f32[256,512]{1,0:T(8,128)}, u32[]{:S(2)}) copy-start(f32[256,512]{1,0:T(8,128)} %get-tuple-element.53.refs_6_) | copy-start | bytes 1572868
  214.6 150.5 %copy-start.12 = (f32[512]{0:T(512)S(1)}, f32[512]{0:T(512)}, u32[]{:S(2)}) copy-start(f32[512]{0:T(512)} %param.23) | copy-start | bytes 6148
  365.2 2.5 copy-start.11
  365.2 3.7 copy-start.5
  365.2 3.7 copy-start.6
  367.7 2.3 copy-start.7
  367.7 2.3 copy-start.8
  367.7 2.3 copy-start.9
  367.7 2.3 copy-start.10
  371.3 1.8 copy-start.4
  373.0 2.2 copy-start.2
  373.0 2.8 copy-start.3
